TPU v7x, 16 devices: a 4x2x1 block of a 4x4x8 slice. The times are simulated.
16 devices in a mesh: dp: 2 (over y, z), tp: 8 (over x, core).
Axes of the slice: x: 4, y: 2, z: 1, core: 2. Of those that a mesh axis runs over, the one named last changes fastest.
The devices are a block of a 4x4x8 slice.
Arguments:
- hidden: bfloat16 [320, 512], P('dp'), parts along dimension 0
- positions: int32 [320], P('dp'), parts along dimension 0
- self_keys: bfloat16 [2, 320, 448, 8, 64], P(None, 'dp', None, 'tp'), parts along dimension 1
- self_vals: bfloat16 [2, 320, 448, 8, 64], P(None, 'dp', None, 'tp'), parts along dimension 1
- cross_keys: bfloat16 [2, 64, 1500, 8, 64], P(None, 'dp', None, 'tp'), parts along dimension 1
- cross_vals: bfloat16 [2, 64, 1500, 8, 64], P(None, 'dp', None, 'tp'), parts along dimension 1
- ln_gain: bfloat16 [2, 3, 512], replicated
- ln_bias: bfloat16 [2, 3, 512], replicated
- w_query: bfloat16 [2, 512, 512], P(None, None, 'tp')
- b_query: bfloat16 [2, 512], P(None, 'tp')
- w_key: bfloat16 [2, 512, 512], P(None, None, 'tp')
- w_value: bfloat16 [2, 512, 512], P(None, None, 'tp')
- b_value: bfloat16 [2, 512], P(None, 'tp')
- w_out: bfloat16 [2, 512, 512], P(None, 'tp')
- b_out: bfloat16 [2, 512], replicated
- w_cquery: bfloat16 [2, 512, 512], P(None, None, 'tp')
- b_cquery: bfloat16 [2, 512], P(None, 'tp')
- w_cout: bfloat16 [2, 512, 512], P(None, 'tp')
- b_cout: bfloat16 [2, 512], replicated
- w_fc1: bfloat16 [2, 512, 2048], P(None, None, 'tp')
- b_fc1: bfloat16 [2, 2048], P(None, 'tp')
- w_fc2: bfloat16 [2, 2048, 512], P(None, 'tp')
- b_fc2: bfloat16 [2, 512], replicated
Outputs:
- output 1: bfloat16 [320, 512], P('dp'), parts along dimension 0
- output 2: bfloat16 [2, 320, 448, 8, 64], P(None, 'dp', None, 'tp'), parts along dimension 1
- output 3: bfloat16 [2, 320, 448, 8, 64], P(None, 'dp', None, 'tp'), parts along dimension 1
There are 2 independent parts. A program takes and returns all parts, laid end to end along the dimension named above; an argument that names none is the same for every part.
All inputs are finite; a program needn't handle non-finite values.
Results may differ from a plain program's by a relative error of at most 0.02.
Values are sent between devices in bfloat16 or wider.
A program may use at most 768 MiB of HBM per device.

v0:
```python
import jax
import jax.numpy as jnp
from jax import lax
from jax.sharding import PartitionSpec as P

EPS = 1e-5
PARAM_NAMES = ('ln_gain', 'ln_bias', 'w_query', 'b_query', 'w_key', 'w_value', 'b_value', 'w_out', 'b_out', 'w_cquery', 'b_cquery', 'w_cout', 'b_cout', 'w_fc1', 'b_fc1', 'w_fc2', 'b_fc2')


def layer_norm(values, gain_row, bias_row):
    wide_vals = values.astype(jnp.float32)
    center = wide_vals - jnp.mean(wide_vals, axis=-1, keepdims=True)
    var_est = jnp.mean(center * center, axis=-1, keepdims=True)
    return (center * lax.rsqrt(var_est + EPS) * gain_row + bias_row).astype(jnp.bfloat16)


def tp_sum(part_out):
    return lax.psum(part_out.astype(jnp.bfloat16), 'tp')


def decoder_layer(hidden, positions, cache_k, cache_v, cross_k, cross_v, layer_w, group_sum):
    batch_size = hidden.shape[0]
    head_count = cache_k.shape[2]
    head_dim = cache_k.shape[3]
    audios = cross_k.shape[0]
    beam_count = batch_size // audios
    qk_scale = head_dim ** -0.25
    slot_ids = lax.broadcasted_iota(jnp.int32, (1, cache_k.shape[1]), 1)
    slot_hit = (slot_ids == positions[:, None])[:, :, None, None]
    slot_mask = (slot_ids <= positions[:, None])[:, None, :]

    normed = layer_norm(hidden, layer_w['ln_gain'][0], layer_w['ln_bias'][0])
    query_heads = ((jnp.dot(normed, layer_w['w_query'], preferred_element_type=jnp.float32) + layer_w['b_query']) * qk_scale).astype(jnp.bfloat16).reshape(batch_size, head_count, head_dim)
    new_key = (jnp.dot(normed, layer_w['w_key'], preferred_element_type=jnp.float32) * qk_scale).astype(jnp.bfloat16).reshape(batch_size, 1, head_count, head_dim)
    new_val = (jnp.dot(normed, layer_w['w_value'], preferred_element_type=jnp.float32) + layer_w['b_value']).astype(jnp.bfloat16).reshape(batch_size, 1, head_count, head_dim)
    cache_k = jnp.where(slot_hit, new_key, cache_k)
    cache_v = jnp.where(slot_hit, new_val, cache_v)
    raw_scores = jnp.einsum('bhd,bshd->bhs', query_heads, cache_k, preferred_element_type=jnp.float32)
    attn_probs = jax.nn.softmax(jnp.where(slot_mask, raw_scores, -1e30), axis=-1).astype(jnp.bfloat16)
    attn_out = jnp.einsum('bhs,bshd->bhd', attn_probs, cache_v, preferred_element_type=jnp.float32).astype(jnp.bfloat16).reshape(batch_size, head_count * head_dim)
    attn_sum = group_sum(jnp.dot(attn_out, layer_w['w_out'], preferred_element_type=jnp.float32))
    hidden = (hidden.astype(jnp.float32) + attn_sum + layer_w['b_out']).astype(jnp.bfloat16)

    normed = layer_norm(hidden, layer_w['ln_gain'][1], layer_w['ln_bias'][1])
    cross_query = ((jnp.dot(normed, layer_w['w_cquery'], preferred_element_type=jnp.float32) + layer_w['b_cquery']) * qk_scale).astype(jnp.bfloat16).reshape(audios, beam_count, head_count, head_dim)
    cross_scores = jnp.einsum('abhd,afhd->abhf', cross_query, cross_k, preferred_element_type=jnp.float32)
    cross_probs = jax.nn.softmax(cross_scores, axis=-1).astype(jnp.bfloat16)
    cross_out = jnp.einsum('abhf,afhd->abhd', cross_probs, cross_v, preferred_element_type=jnp.float32).astype(jnp.bfloat16).reshape(batch_size, head_count * head_dim)
    cross_sum = group_sum(jnp.dot(cross_out, layer_w['w_cout'], preferred_element_type=jnp.float32))
    hidden = (hidden.astype(jnp.float32) + cross_sum + layer_w['b_cout']).astype(jnp.bfloat16)

    normed = layer_norm(hidden, layer_w['ln_gain'][2], layer_w['ln_bias'][2])
    mlp_inner = jax.nn.gelu(jnp.dot(normed, layer_w['w_fc1'], preferred_element_type=jnp.float32) + layer_w['b_fc1'], approximate=False).astype(jnp.bfloat16)
    mlp_sum = group_sum(jnp.dot(mlp_inner, layer_w['w_fc2'], preferred_element_type=jnp.float32))
    hidden = (hidden.astype(jnp.float32) + mlp_sum + layer_w['b_fc2']).astype(jnp.bfloat16)
    return hidden, cache_k, cache_v


def solution(mesh):
    cache_spec = P(None, 'dp', None, 'tp', None)
    col_spec = P(None, None, 'tp')
    row_spec = P(None, 'tp', None)
    vec_spec = P(None, 'tp')
    param_specs = {'ln_gain': P(), 'ln_bias': P(), 'w_query': col_spec, 'b_query': vec_spec, 'w_key': col_spec, 'w_value': col_spec, 'b_value': vec_spec, 'w_out': row_spec, 'b_out': P(), 'w_cquery': col_spec, 'b_cquery': vec_spec, 'w_cout': row_spec, 'b_cout': P(), 'w_fc1': col_spec, 'b_fc1': vec_spec, 'w_fc2': row_spec, 'b_fc2': P()}
    in_specs = (P('dp', None), P('dp'), cache_spec, cache_spec, cache_spec, cache_spec) + tuple(param_specs[param_name] for param_name in PARAM_NAMES)

    def local_step(hidden, positions, self_keys, self_vals, cross_keys, cross_vals, *layer_params):
        keys_out = []
        vals_out = []
        for layer_idx in range(self_keys.shape[0]):
            layer_w = {param_name: stacked[layer_idx] for param_name, stacked in zip(PARAM_NAMES, layer_params)}
            hidden, cache_k, cache_v = decoder_layer(hidden, positions, self_keys[layer_idx], self_vals[layer_idx], cross_keys[layer_idx], cross_vals[layer_idx], layer_w, tp_sum)
            keys_out.append(cache_k)
            vals_out.append(cache_v)
        return hidden, jnp.stack(keys_out), jnp.stack(vals_out)

    return jax.shard_map(local_step, mesh=mesh, in_specs=in_specs, out_specs=(P('dp', None), cache_spec, cache_spec), check_vma=False)
```

profile of v0, /device:TPU:113, one launch (start us, length us, event | category | flops | bytes accessed | tf_op | source)
XLA Modules:
  0.0 414.1 jit_solution(10586690507675749978)
XLA Ops:
  8.3 1.1 fusion.78
  13.3 1.1 fusion.81
  17.8 5.1 %fusion.3 = f32[160,1,448]{2,1,0:T(1,128)S(1)} fusion(bf16[160,64,1]{1,2,0:T(2,128)(2,1)S(1)} %copy.66, pred[160,448]{1,0:T(8,128)(4,1)S(1)} %iota_compare_fusion, bf16[2,160,448,1,64]{2,4,1,3,0:T(8,128)(2,1)} %bitcast.225, bf16[160,64]{1,0:T(8,128)(2,1)S(1)} %copy.46), kind=kOutput, calls=%fused_computation.10 | convolution fusion | flops 13762560 | bytes 10885120 | tf_op jit(solution)/shard_map/bhd,bshd->bhs/dot_general | solution.py:38
  23.5 4.3 %copy-done = bf16[2,160,448,1,64]{2,4,3,1,0:T(8,128)(2,1)S(1)} copy-done((bf16[2,160,448,1,64]{2,4,3,1,0:T(8,128)(2,1)S(1)}, bf16[2,160,448,1,64]{2,4,3,1,0:T(8,128)(2,1)}, u32[]{:S(2)}) %copy-start) | copy-done | bytes 18350104
  27.8 3.7 fusion.2
  32.5 52.4 %all-reduce.7.cloned.1.call-done = bf16[160,512]{1,0:T(8,128)(2,1)} async-done(((bf16[160,512]{1,0:T(8,128)(2,1)}), bf16[160,512]{1,0:T(8,128)(2,1)}) %all-reduce.7.cloned.1.call-update) | async-done | bytes 163856 | tf_op jit(solution)/shard_map/psum | solution.py:18
  86.7 3.9 fusion.319
  91.0 4.6 %fusion.27 = bf16[32,5,1,64]{3,1,0,2:T(8,128)(2,1)S(1)} fusion(bf16[2,32,1500,1,64]{2,4,1,3,0:T(8,128)(2,1)} %bitcast.256, f32[32,5,1,1500]{3,1,0,2:T(8,128)S(1)} %get-tuple-element.49, f32[32,5]{1,0:T(8,128)S(1)} %fusion.22, f32[32,5]{1,0:T(8,128)S(1)} %get-tuple-element.48), kind=kOutput, calls=%fused_computation.53 | convolution fusion | flops 31450240 | bytes 7273216 | tf_op jit(solution)/shard_map/abhf,afhd->abhd/dot_general | solution.py:48
  96.7 50.8 %all-reduce.9.cloned.1.call-done = bf16[160,512]{1,0:T(8,128)(2,1)} async-done(((bf16[160,512]{1,0:T(8,128)(2,1)}), bf16[160,512]{1,0:T(8,128)(2,1)}) %all-reduce.9.cloned.1.call-update) | async-done | bytes 163856 | tf_op jit(solution)/shard_map/psum | solution.py:18
  148.8 1.5 convolution_convert_fusion.1
  150.4 50.8 %all-reduce.11.cloned.1.call-done = bf16[160,512]{1,0:T(8,128)(2,1)} async-done(((bf16[160,512]{1,0:T(8,128)(2,1)}), bf16[160,512]{1,0:T(8,128)(2,1)}) %all-reduce.11.cloned.1.call-update) | async-done | bytes 163856 | tf_op jit(solution)/shard_map/psum | solution.py:18
  203.6 24.7 %broadcast_select_fusion.1 = (bf16[1,160,448,1,64]{2,4,1,3,0:T(8,128)(2,1)}, bf16[1,160,448,1,64]{2,4,1,3,0:T(8,128)(2,1)}, bf16[1,160,448,1,64]{2,4,3,1,0:T(8,128)(2,1)}) fusion(pred[160,448]{1,0:T(8,128)(4,1)S(1)} %iota_compare_fusion, bf16[2,160,448,1,64]{2,4,1,3,0:T(8,128)(2,1)} %bitcast.226, bf16[160,64]{1,0:T(8,128)(2,1)S(1)} %copy.46, ...), kind=kLoop, calls=%fused_computation.13 | loop fusion | flops 13762560 | bytes 55183360 | tf_op jit(solution)/shard_map/jit(_where)/select_n | solution.py:36
  228.3 5.1 %fusion.1 = f32[160,1,448]{2,1,0:T(1,128)S(1)} fusion(bf16[160,64,1]{1,2,0:T(2,128)(2,1)S(1)} %copy.70, pred[160,448]{1,0:T(8,128)(4,1)S(1)} %iota_compare_fusion, bf16[2,160,448,1,64]{2,4,1,3,0:T(8,128)(2,1)} %bitcast.227, bf16[160,64]{1,0:T(8,128)(2,1)S(1)} %copy.53), kind=kOutput, calls=%fused_computation.6 | convolution fusion | flops 13762560 | bytes 10885120 | tf_op jit(solution)/shard_map/bhd,bshd->bhs/dot_general | solution.py:38
  234.1 3.7 fusion
  238.9 10.3 %bitcast_select_fusion = bf16[1,160,448,1,64]{2,4,3,1,0:T(8,128)(2,1)} fusion(pred[160,448]{1,0:T(8,128)(4,1)S(1)} %iota_compare_fusion, bf16[2,160,448,1,64]{2,4,3,1,0:T(8,128)(2,1)} %param.26, bf16[160,64]{1,0:T(8,128)(2,1)S(1)} %copy.55), kind=kLoop, calls=%fused_computation.2 | loop fusion | flops 4587520 | bytes 18442240 | tf_op jit(solution)/shard_map/jit(_where)/select_n | solution.py:37
  249.2 40.4 %all-reduce.13.cloned.1.call-done = bf16[160,512]{1,0:T(8,128)(2,1)} async-done(((bf16[160,512]{1,0:T(8,128)(2,1)}), bf16[160,512]{1,0:T(8,128)(2,1)}) %all-reduce.13.cloned.1.call-update) | async-done | bytes 163856 | tf_op jit(solution)/shard_map/psum | solution.py:18
  291.3 3.8 fusion.320
  295.5 4.6 %fusion.26 = bf16[32,5,1,64]{3,1,0,2:T(8,128)(2,1)S(1)} fusion(bf16[2,32,1500,1,64]{2,4,1,3,0:T(8,128)(2,1)} %bitcast.257, f32[32,5,1,1500]{3,1,0,2:T(8,128)S(1)} %get-tuple-element.51, f32[32,5]{1,0:T(8,128)S(1)} %fusion.23, f32[32,5]{1,0:T(8,128)S(1)} %get-tuple-element.50), kind=kOutput, calls=%fused_computation.52 | convolution fusion | flops 31450240 | bytes 7273216 | tf_op jit(solution)/shard_map/abhf,afhd->abhd/dot_general | solution.py:48
  301.1 17.4 %maximum_bitcast_fusion = bf16[2,160,448,1,64]{2,4,3,1,0:T(8,128)(2,1)} fusion(bf16[1,160,448,1,64]{2,4,1,3,0:T(8,128)(2,1)} %get-tuple-element.20, bf16[1,160,448,1,64]{2,4,1,3,0:T(8,128)(2,1)} %get-tuple-element.19), kind=kLoop, calls=%fused_computation | loop fusion | flops 9175040 | bytes 36700160
  318.4 33.5 %all-reduce.15.cloned.1.call-done = bf16[160,512]{1,0:T(8,128)(2,1)} async-done(((bf16[160,512]{1,0:T(8,128)(2,1)}), bf16[160,512]{1,0:T(8,128)(2,1)}) %all-reduce.15.cloned.1.call-update) | async-done | bytes 163856 | tf_op jit(solution)/shard_map/psum | solution.py:18
  353.2 1.5 convolution_convert_fusion
  354.7 17.4 %pad_maximum_fusion = bf16[2,160,448,1,64]{2,4,3,1,0:T(8,128)(2,1)} fusion(bf16[1,160,448,1,64]{2,4,3,1,0:T(8,128)(2,1)} %bitcast_select_fusion, bf16[1,160,448,1,64]{2,4,3,1,0:T(8,128)(2,1)} %get-tuple-element.21), kind=kLoop, calls=%fused_computation.1 | loop fusion | flops 9175040 | bytes 36700160 | tf_op jit(solution)/shard_map/stack | solution.py:75
  372.1 33.5 %all-reduce.17.cloned.1.call-done = bf16[160,512]{1,0:T(8,128)(2,1)} async-done(((bf16[160,512]{1,0:T(8,128)(2,1)}), bf16[160,512]{1,0:T(8,128)(2,1)}) %all-reduce.17.cloned.1.call-update) | async-done | bytes 163856 | tf_op jit(solution)/shard_map/psum | solution.py:18
  405.6 1.6 fusion.93
  (120 shorter events, 23.0 us)
Async XLA Ops:
  7.2 77.8 %all-reduce.7.cloned.1.call-start = ((), (), s32[]{:S(2)}) async-start(), calls=%async_computation | async-start | bytes 327680 | tf_op jit(solution)/shard_map/psum | solution.py:18
  17.7 5.1 %copy-start.5 = (s32[160]{0:T(256)S(1)}, s32[160]{0:T(256)}, u32[]{:S(2)}) copy-start(s32[160]{0:T(256)} %param.24) | copy-start | bytes 1924
  17.8 10.0 %copy-start = (bf16[2,160,448,1,64]{2,4,3,1,0:T(8,128)(2,1)S(1)}, bf16[2,160,448,1,64]{2,4,3,1,0:T(8,128)(2,1)}, u32[]{:S(2)}) copy-start(bf16[2,160,448,1,64]{2,4,3,1,0:T(8,128)(2,1)} %param.26) | copy-start | bytes 55050244
  27.8 4.7 %copy-start.10 = (bf16[2,64]{1,0:T(2,128)(2,1)S(1)}, bf16[2,64]{1,0:T(2,128)(2,1)}, u32[]{:S(2)}) copy-start(bf16[2,64]{1,0:T(2,128)(2,1)} %param.39) | copy-start | bytes 772
  27.8 57.2 %copy-start.1 = (bf16[160,512]{1,0:T(8,128)(2,1)S(1)}, bf16[160,512]{1,0:T(8,128)(2,1)}, u32[]{:S(2)}) copy-start(bf16[160,512]{1,0:T(8,128)(2,1)} %param.23) | copy-start | bytes 491524
  27.8 58.4 %copy-start.15 = (bf16[2,512,64]{1,2,0:T(8,128)(2,1)S(1)}, bf16[2,512,64]{1,2,0:T(8,128)(2,1)}, u32[]{:S(2)}) copy-start(bf16[2,512,64]{1,2,0:T(8,128)(2,1)} %param.38) | copy-start | bytes 393220
  32.4 115.1 %all-reduce.9.cloned.1.call-start = ((), (), s32[]{:S(2)}) async-start(), calls=%async_computation.1 | async-start | bytes 327680 | tf_op jit(solution)/shard_map/psum | solution.py:18
  86.7 9.0 %copy-start.4 = (bf16[2,64,512]{2,1,0:T(8,128)(2,1)S(1)}, bf16[2,64,512]{2,1,0:T(8,128)(2,1)}, u32[]{:S(2)}) copy-start(bf16[2,64,512]{2,1,0:T(8,128)(2,1)} %param.40) | copy-start | bytes 393220
  86.7 10.0 %copy-start.9 = (bf16[2,256]{1,0:T(2,128)(2,1)S(1)}, bf16[2,256]{1,0:T(2,128)(2,1)}, u32[]{:S(2)}) copy-start(bf16[2,256]{1,0:T(2,128)(2,1)} %param.43) | copy-start | bytes 3076
  86.7 62.1 %copy-start.11 = (bf16[2,256,512]{2,1,0:T(8,128)(2,1)S(1)}, bf16[2,256,512]{2,1,0:T(8,128)(2,1)}, u32[]{:S(2)}) copy-start(bf16[2,256,512]{2,1,0:T(8,128)(2,1)} %param.44) | copy-start | bytes 1572868
  86.7 62.1 %copy-start.12 = (bf16[2,512,256]{2,1,0:T(8,128)(2,1)S(1)}, bf16[2,512,256]{2,1,0:T(8,128)(2,1)}, u32[]{:S(2)}) copy-start(bf16[2,512,256]{2,1,0:T(8,128)(2,1)} %param.42) | copy-start | bytes 1572868
  90.6 59.8 %copy-start.8 = (bf16[2,512]{1,0:T(2,128)(2,1)S(1)}, bf16[2,512]{1,0:T(2,128)(2,1)}, u32[]{:S(2)}) copy-start(bf16[2,512]{1,0:T(2,128)(2,1)} %param.45) | copy-start | bytes 6148
  90.6 112.0 %copy-start.3 = (bf16[2,512,64]{1,2,0:T(8,128)(2,1)S(1)}, bf16[2,512,64]{1,2,0:T(8,128)(2,1)}, u32[]{:S(2)}) copy-start(bf16[2,512,64]{1,2,0:T(8,128)(2,1)} %param.33) | copy-start | bytes 393220
  91.0 111.8 %copy-start.13 = (bf16[2,512,64]{1,2,0:T(8,128)(2,1)S(1)}, bf16[2,512,64]{1,2,0:T(8,128)(2,1)}, u32[]{:S(2)}) copy-start(bf16[2,512,64]{1,2,0:T(8,128)(2,1)} %param.34) | copy-start | bytes 393220
  91.0 112.1 %copy-start.14 = (bf16[2,512,64]{1,2,0:T(8,128)(2,1)S(1)}, bf16[2,512,64]{1,2,0:T(8,128)(2,1)}, u32[]{:S(2)}) copy-start(bf16[2,512,64]{1,2,0:T(8,128)(2,1)} %param.31) | copy-start | bytes 393220
  96.6 104.6 %all-reduce.11.cloned.1.call-start = ((), (), s32[]{:S(2)}) async-start(), calls=%async_computation.2 | async-start | bytes 327680 | tf_op jit(solution)/shard_map/psum | solution.py:18
  150.3 139.3 %all-reduce.13.cloned.1.call-start = ((), (), s32[]{:S(2)}) async-start(), calls=%async_computation.3 | async-start | bytes 327680 | tf_op jit(solution)/shard_map/psum | solution.py:18
  203.5 30.5 %slice-start = ((s8[20971520]{0:T(1024)(128)(4,1)}), s8[4194304]{0:T(1024)(128)(4,1)S(1)}, s32[]{:S(2)}) async-start(s8[20971520]{0:T(1024)(128)(4,1)} %bitcast.230), calls=%async_computation.6 | async-start | bytes 8388608
  203.6 30.5 %slice-start.1 = ((s8[20971520]{0:T(1024)(128)(4,1)}), s8[4194304]{0:T(1024)(128)(4,1)S(1)}, s32[]{:S(2)}) async-start(s8[20971520]{0:T(1024)(128)(4,1)} %bitcast.230), calls=%async_computation.7 | async-start | bytes 8388608
  203.6 30.5 %slice-start.2 = ((s8[20971520]{0:T(1024)(128)(4,1)}), s8[4194304]{0:T(1024)(128)(4,1)S(1)}, s32[]{:S(2)}) async-start(s8[20971520]{0:T(1024)(128)(4,1)} %bitcast.230), calls=%async_computation.8 | async-start | bytes 8388608
  203.6 30.5 %slice-start.3 = ((s8[20971520]{0:T(1024)(128)(4,1)}), s8[4194304]{0:T(1024)(128)(4,1)S(1)}, s32[]{:S(2)}) async-start(s8[20971520]{0:T(1024)(128)(4,1)} %bitcast.230), calls=%async_computation.9 | async-start | bytes 8388608
  228.3 5.8 %slice-start.4 = ((s8[20971520]{0:T(1024)(128)(4,1)}), s8[4194304]{0:T(1024)(128)(4,1)S(1)}, s32[]{:S(2)}) async-start(s8[20971520]{0:T(1024)(128)(4,1)} %bitcast.230), calls=%async_computation.10 | async-start | bytes 8388608
  238.7 113.2 %all-reduce.15.cloned.1.call-start = ((), (), s32[]{:S(2)}) async-start(), calls=%async_computation.4 | async-start | bytes 327680 | tf_op jit(solution)/shard_map/psum | solution.py:18
  301.0 104.6 %all-reduce.17.cloned.1.call-start = ((), (), s32[]{:S(2)}) async-start(), calls=%async_computation.5 | async-start | bytes 327680 | tf_op jit(solution)/shard_map/psum | solution.py:18
  (3 other events, 13.1 us)
Sparse Core Ops, SparseCore 0:
  32.5 52.3 all-reduce.6
  96.7 50.7 all-reduce.8
  150.4 50.7 all-reduce.10
  238.8 50.7 all-reduce.12
  301.1 50.7 all-reduce.14
  354.8 50.7 all-reduce.16
where the time goes:
time: 416 us; the launch traced here: 414 us
  waiting for transfers between devices  262 us (63%)
  other arithmetic  86.9 us (21%)
  matrix products  44.8 us (11%)
  between operations  14.6 us (4%)
  local copies, waits for them, and re-layouts  5.43 us (1%)
    psum x6, waiting for transfers between devices, tp_sum(): return lax.psum(part_out.astype(jnp.bfloat16), 'tp')  261 us
    select_n x1, other arithmetic, decoder_layer(): cache_k = jnp.where(slot_hit, new_key, cache_k)  24.7 us
    unnamed x2, other arithmetic  17.4 us
    another operation x1, other arithmetic, local_step(): return (hidden, jnp.stack(keys_out), jnp.stack(vals_out))  17.4 us
    select_n x1, other arithmetic, decoder_layer(): cache_v = jnp.where(slot_hit, new_val, cache_v)  10.3 us
    dot_general x2, matrix products, decoder_layer(): jnp.einsum('bhd,bshd->bhs', query_heads, cache_k, preferred_element_type=...  10.2 us
    dot_general x2, matrix products, decoder_layer(): jnp.einsum('abhf,afhd->abhd', cross_probs, cross_v, preferred_element_typ...  9.19 us
  transfers between devices with their start and end apart: 6, of which 6 were waited for; matrix products, arithmetic and copies ran while one was open for 11% of the time, Pallas kernels for 0%

commit v1 on v0

v1 whole, which is shorter than its diff:
```python
import functools

import jax
import jax.numpy as jnp
from jax import lax
from jax.experimental import pallas as pl
from jax.experimental.pallas import tpu as pltpu
from jax.sharding import PartitionSpec as P

EPS = 1e-5
NEG = -1e30
PARAM_NAMES = ('ln_gain', 'ln_bias', 'w_query', 'b_query', 'w_key', 'w_value', 'b_value', 'w_out', 'b_out', 'w_cquery', 'b_cquery', 'w_cout', 'b_cout', 'w_fc1', 'b_fc1', 'w_fc2', 'b_fc2')
F32 = jnp.float32
BF16 = jnp.bfloat16
VMEM = pltpu.VMEM
NT = (((1,), (1,)), ((), ()))


def dot(a, b):
    return jnp.dot(a, b, preferred_element_type=F32)


def dot_nt(a, b):
    return lax.dot_general(a, b, NT, preferred_element_type=F32)


def layer_norm(wide_vals, gain_row, bias_row):
    center = wide_vals - jnp.mean(wide_vals, axis=-1, keepdims=True)
    var_est = jnp.mean(center * center, axis=-1, keepdims=True)
    return (center * lax.rsqrt(var_est + EPS) * gain_row + bias_row).astype(BF16)


def iota(shape, dim):
    return lax.broadcasted_iota(jnp.int32, shape, dim)


def stack_eye(rows, width):
    return (iota((width, rows), 1) % width == iota((width, rows), 0)).astype(BF16)


def row(ref, *idx):
    return ref[idx].astype(F32)


def self_kernel(layer, group, pos_ref, hidden_ref, gain_ref, bias_ref, wq_ref, bq_ref, wk_ref, wv_ref, bv_ref, kin_ref, vin_ref, *rest):
    o_ref, kout_ref, vout_ref, kbuf, vbuf, qbd, kcol, vcol, osc, in_sem, out_sem = rest[-11:]
    batch = hidden_ref.shape[0]
    head = wq_ref.shape[1]
    slots = kbuf.shape[2]
    groups = batch // group
    span = group * head
    base = layer * batch * head
    scale = head ** -0.25

    def in_copy(src, buf, which, g):
        return pltpu.make_async_copy(src.at[pl.ds(base + g * span, span), :], buf.at[g], in_sem.at[which, g])

    def out_copy(buf, dst, which, g):
        return pltpu.make_async_copy(buf.at[g], dst.at[pl.ds(base + g * span, span), :], out_sem.at[which, g])

    def start(g, carry):
        in_copy(kin_ref, kbuf, 0, g).start()
        in_copy(vin_ref, vbuf, 1, g).start()
        return carry

    lax.fori_loop(0, groups, start, 0)

    normed = layer_norm(hidden_ref[...].astype(F32), gain_ref[0, layer:layer + 1, :].astype(F32), bias_ref[0, layer:layer + 1, :].astype(F32))
    q = ((dot_nt(normed, wq_ref[layer]) + bq_ref[layer:layer + 1, :].astype(F32)) * scale).astype(BF16)
    k = (dot_nt(normed, wk_ref[layer]) * scale).astype(BF16)
    v = (dot_nt(normed, wv_ref[layer]) + bv_ref[layer:layer + 1, :].astype(F32)).astype(BF16)
    eye = stack_eye(span, head)
    wide_q = dot(q, eye)
    diag = iota((batch, span), 0) % group == iota((batch, span), 1) // head
    qbd[...] = jnp.where(diag, wide_q, 0.0)
    k_t = k.astype(F32).T
    v_t = v.astype(F32).T
    for g in range(groups):
        kcol[g] = k_t[:, g * group:(g + 1) * group]
        vcol[g] = v_t[:, g * group:(g + 1) * group]

    lane_ids = iota((group, slots), 1)
    row_ids = iota((group, slots), 0)
    odiag = iota((span, group), 0) // head == iota((span, group), 1)
    full_tiles = slots // 128
    tail = slots - full_tiles * 128

    def attend(g, carry):
        in_copy(kin_ref, kbuf, 0, g).wait()
        in_copy(vin_ref, vbuf, 1, g).wait()
        kc = kcol[g]
        vc = vcol[g]
        limit = jnp.zeros((group, slots), jnp.int32)
        for i in range(group):
            pos = pos_ref[g * group + i]
            limit = jnp.where(row_ids == i, pos, limit)
            tile = pos // 128
            local = pos - tile * 128
            rows = slice(i * head, (i + 1) * head)

            def put(cols, width):
                hit = iota((head, width), 1) == local
                for buf, col in ((kbuf, kc), (vbuf, vc)):
                    old = buf[g, rows, cols].astype(F32)
                    buf[g, rows, cols] = jnp.where(hit, col[:, i:i + 1], old).astype(BF16)

            @pl.when(tile < full_tiles)
            def _():
                put(pl.ds(pl.multiple_of(tile * 128, 128), 128), 128)

            @pl.when(tile >= full_tiles)
            def _():
                put(slice(full_tiles * 128, slots), tail)

        out_copy(kbuf, kout_ref, 0, g).start()
        out_copy(vbuf, vout_ref, 1, g).start()
        scores = dot(qbd[pl.ds(pl.multiple_of(g * group, group), group), :].astype(BF16), kbuf[g])
        scores = jnp.where(lane_ids <= limit, scores, NEG)
        probs = jnp.exp(scores - jnp.max(scores, axis=-1, keepdims=True))
        probs = (probs / jnp.sum(probs, axis=-1, keepdims=True)).astype(BF16)
        wide_o = dot_nt(vbuf[g], probs)
        o_t = dot(eye, jnp.where(odiag, wide_o, 0.0).astype(BF16))
        osc[pl.ds(pl.multiple_of(g * group, group), group), :] = o_t.T
        return carry

    lax.fori_loop(0, groups, attend, 0)
    o_ref[...] = osc[...].astype(BF16)

    def finish(g, carry):
        out_copy(kbuf, kout_ref, 0, g).wait()
        out_copy(vbuf, vout_ref, 1, g).wait()
        return carry

    lax.fori_loop(0, groups, finish, 0)


def self_attention(layer, hidden, positions, keys, vals, prev, params):
    batch = hidden.shape[0]
    head = params['w_query'].shape[1]
    slots = keys.shape[1]
    group = 8
    groups = batch // group
    any_spec = pl.BlockSpec(memory_space=pltpu.HBM)
    vm = pl.BlockSpec(memory_space=VMEM)
    operands = [positions, hidden, params['ln_gain'], params['ln_bias'], params['w_query'], params['b_query'], params['w_key'], params['w_value'], params['b_value'], keys, vals]
    in_specs = [pl.BlockSpec(memory_space=pltpu.SMEM)] + [vm] * 8 + [any_spec] * 2
    aliases = {}
    if prev is not None:
        operands += list(prev)
        in_specs += [any_spec] * 2
        aliases = {11: 1, 12: 2}
    return pl.pallas_call(
        functools.partial(self_kernel, layer, group),
        out_shape=(jax.ShapeDtypeStruct((batch, head), BF16), jax.ShapeDtypeStruct(keys.shape, BF16), jax.ShapeDtypeStruct(vals.shape, BF16)),
        in_specs=in_specs,
        out_specs=(vm, any_spec, any_spec),
        scratch_shapes=[
            VMEM((groups, group * head, slots), BF16),
            VMEM((groups, group * head, slots), BF16),
            VMEM((batch, group * head), F32),
            VMEM((groups, head, group), F32),
            VMEM((groups, head, group), F32),
            VMEM((batch, head), F32),
            pltpu.SemaphoreType.DMA((2, groups)),
            pltpu.SemaphoreType.DMA((2, groups)),
        ],
        input_output_aliases=aliases,
        compiler_params=pltpu.CompilerParams(vmem_limit_bytes=40 * 2**20),
        name='self_attention',
    )(*operands)


def cross_kernel(layer, tp, group, o_ref, hidden_ref, gain_ref, bias_ref, wo_ref, bo_ref, wcq_ref, bcq_ref, wco_ref, bco_ref, w1_ref, b1_ref, w2_ref, b2_ref, kin_ref, vin_ref, hidden_out_ref, kbuf, vbuf, part, landed, blocks, qbd, osc, in_sem, rs_send, rs_recv, ag_send, ag_recv):
    me = lax.axis_index('tp')
    batch, width = hidden_ref.shape
    head = wcq_ref.shape[1]
    half = batch // 2
    quarters = width // 128
    chunks = kbuf.shape[0]
    span = kbuf.shape[1]
    base = layer * chunks * span
    scale = head ** -0.25
    beams = batch // (chunks * group)
    rows = group * beams

    def in_copy(src, buf, which, c):
        return pltpu.make_async_copy(src.at[pl.ds(base + c * span, span), :], buf.at[c], in_sem.at[which, c])

    for c in range(chunks):
        in_copy(kin_ref, kbuf, 0, c).start()
        in_copy(vin_ref, vbuf, 1, c).start()

    barrier = pltpu.get_barrier_semaphore()
    peers = [lax.rem(me + step, tp) for step in range(1, tp)]
    for peer in peers:
        pl.semaphore_signal(barrier, inc=1, device_id={'tp': peer}, device_id_type=pl.DeviceIdType.MESH)

    def bounds(j):
        r, c = j // quarters, j % quarters
        return slice(r * half, (r + 1) * half), slice(c * 128, (c + 1) * 128)

    for j in range(tp):
        rs, cs = bounds(j)
        blocks[0, j] = hidden_ref[rs, cs]

    def exchange(x, total, bias_ref, entry):
        for j in range(tp):
            rs, cs = bounds(j)
            part[x, j] = total[rs, cs].astype(BF16)
        if entry:
            pl.semaphore_wait(barrier, tp - 1)
        sends = []
        for n, peer in enumerate(peers):
            copy = pltpu.make_async_remote_copy(part.at[x, peer], landed.at[x, me], rs_send.at[x, n], rs_recv.at[x, me], device_id={'tp': peer}, device_id_type=pl.DeviceIdType.MESH)
            copy.start()
            sends.append(copy)
        bias = bias_ref[layer:layer + 1, :].astype(F32)
        own = lax.rem(me, quarters)
        bias_row = jnp.zeros((1, 128), F32)
        for c in range(quarters):
            bias_row = jnp.where(own == c, bias[:, c * 128:(c + 1) * 128], bias_row)
        acc = part[x, me].astype(F32)
        for peer in reversed(peers):
            pltpu.make_async_remote_copy(part.at[x, peer], landed.at[x, peer], rs_send.at[x, 0], rs_recv.at[x, peer], device_id={'tp': peer}, device_id_type=pl.DeviceIdType.MESH).wait_recv()
            acc = acc + landed[x, peer].astype(F32)
        blocks[x + 1, me] = (blocks[x, me].astype(F32) + acc + bias_row).astype(BF16)
        for n, peer in enumerate(peers):
            copy = pltpu.make_async_remote_copy(blocks.at[x + 1, me], blocks.at[x + 1, me], ag_send.at[x, n], ag_recv.at[x, me], device_id={'tp': peer}, device_id_type=pl.DeviceIdType.MESH)
            copy.start()
            sends.append(copy)
        for peer in peers:
            pltpu.make_async_remote_copy(blocks.at[x + 1, peer], blocks.at[x + 1, peer], ag_send.at[x, 0], ag_recv.at[x, peer], device_id={'tp': peer}, device_id_type=pl.DeviceIdType.MESH).wait_recv()
        for copy in sends:
            copy.wait_send()

    def whole(x):
        tops = [jnp.concatenate([blocks[x, r * quarters + c] for c in range(quarters)], axis=1) for r in range(tp // quarters)]
        return jnp.concatenate(tops, axis=0)

    exchange(0, dot(o_ref[...], wo_ref[layer]), bo_ref, True)

    normed = layer_norm(whole(1).astype(F32), gain_ref[1, layer:layer + 1, :].astype(F32), bias_ref[1, layer:layer + 1, :].astype(F32))
    q = ((dot_nt(normed, wcq_ref[layer]) + bcq_ref[layer:layer + 1, :].astype(F32)) * scale).astype(BF16)
    eye = stack_eye(span, head)
    diag = (iota((batch, span), 0) // beams) % group == iota((batch, span), 1) // head
    qbd[...] = jnp.where(diag, dot(q, eye), 0.0)
    odiag = iota((span, rows), 0) // head == iota((span, rows), 1) // beams
    for c in range(chunks):
        in_copy(kin_ref, kbuf, 0, c).wait()
        scores = dot(qbd[c * rows:(c + 1) * rows, :].astype(BF16), kbuf[c])
        probs = jnp.exp(scores - jnp.max(scores, axis=-1, keepdims=True))
        probs = (probs / jnp.sum(probs, axis=-1, keepdims=True)).astype(BF16)
        in_copy(vin_ref, vbuf, 1, c).wait()
        wide_o = dot_nt(vbuf[c], probs)
        o_t = dot(eye, jnp.where(odiag, wide_o, 0.0).astype(BF16))
        osc[c * rows:(c + 1) * rows, :] = o_t.T
    exchange(1, dot(osc[...].astype(BF16), wco_ref[layer]), bco_ref, False)

    normed = layer_norm(whole(2).astype(F32), gain_ref[2, layer:layer + 1, :].astype(F32), bias_ref[2, layer:layer + 1, :].astype(F32))
    inner = dot(normed, w1_ref[layer]) + b1_ref[layer:layer + 1, :].astype(F32)
    inner = (0.5 * inner * (1.0 + lax.erf(inner * (0.5 ** 0.5)))).astype(BF16)
    exchange(2, dot(inner, w2_ref[layer]), b2_ref, False)
    hidden_out_ref[...] = whole(3)


def cross_and_mlp(layer, tp, attn_out, hidden, keys, vals, audios, params):
    batch, width = hidden.shape
    head = params['w_cquery'].shape[1]
    frames = keys.shape[1]
    group = 8
    chunks = audios // group
    vm = pl.BlockSpec(memory_space=VMEM)
    any_spec = pl.BlockSpec(memory_space=pltpu.HBM)
    names = ('ln_gain', 'ln_bias', 'w_out', 'b_out', 'w_cquery', 'b_cquery', 'w_cout', 'b_cout', 'w_fc1', 'b_fc1', 'w_fc2', 'b_fc2')
    block = (batch // 2, 128)
    return pl.pallas_call(
        functools.partial(cross_kernel, layer, tp, group),
        out_shape=jax.ShapeDtypeStruct((batch, width), BF16),
        in_specs=[vm] * 14 + [any_spec] * 2,
        out_specs=vm,
        scratch_shapes=[
            VMEM((chunks, group * head, frames), BF16),
            VMEM((chunks, group * head, frames), BF16),
            VMEM((3, tp) + block, BF16),
            VMEM((3, tp) + block, BF16),
            VMEM((4, tp) + block, BF16),
            VMEM((batch, group * head), F32),
            VMEM((batch, head), F32),
            pltpu.SemaphoreType.DMA((2, chunks)),
            pltpu.SemaphoreType.DMA((3, tp - 1)),
            pltpu.SemaphoreType.DMA((3, tp)),
            pltpu.SemaphoreType.DMA((3, tp - 1)),
            pltpu.SemaphoreType.DMA((3, tp)),
        ],
        compiler_params=pltpu.CompilerParams(vmem_limit_bytes=40 * 2**20, collective_id=layer, has_side_effects=True),
        name='cross_and_mlp',
    )(attn_out, hidden, *[params[n] for n in names], keys, vals)


def solution(mesh):
    tp = mesh.shape['tp']
    cache_spec = P(None, 'dp', None, 'tp', None)
    col_spec = P(None, None, 'tp')
    row_spec = P(None, 'tp', None)
    vec_spec = P(None, 'tp')
    param_specs = {'ln_gain': P(), 'ln_bias': P(), 'w_query': col_spec, 'b_query': vec_spec, 'w_key': col_spec, 'w_value': col_spec, 'b_value': vec_spec, 'w_out': row_spec, 'b_out': P(), 'w_cquery': col_spec, 'b_cquery': vec_spec, 'w_cout': row_spec, 'b_cout': P(), 'w_fc1': col_spec, 'b_fc1': vec_spec, 'w_fc2': row_spec, 'b_fc2': P()}
    in_specs = (P('dp', None), P('dp'), cache_spec, cache_spec, cache_spec, cache_spec) + tuple(param_specs[param_name] for param_name in PARAM_NAMES)

    def flat(cache):
        layers, n, slots, heads, head = cache.shape
        return cache.transpose(0, 1, 3, 4, 2).reshape(layers * n * heads * head, slots)

    def local_step(hidden, positions, self_keys, self_vals, cross_keys, cross_vals, *layer_params):
        params = dict(zip(PARAM_NAMES, layer_params))
        for name in ('w_query', 'w_key', 'w_value', 'w_cquery'):
            params[name] = params[name].transpose(0, 2, 1)
        for name in ('ln_gain', 'ln_bias'):
            params[name] = params[name].transpose(1, 0, 2)
        layers, batch, slots, heads, head = self_keys.shape
        audios = cross_keys.shape[1]
        keys, vals, ckeys, cvals = flat(self_keys), flat(self_vals), flat(cross_keys), flat(cross_vals)
        prev = None
        for layer in range(layers):
            attn_out, *prev = self_attention(layer, hidden, positions, keys, vals, prev, params)
            hidden = cross_and_mlp(layer, tp, attn_out, hidden, ckeys, cvals, audios, params)

        def unflat(cache):
            return cache.reshape(layers, batch, heads, head, slots).transpose(0, 1, 4, 2, 3)

        return hidden, unflat(prev[0]), unflat(prev[1])

    return jax.shard_map(local_step, mesh=mesh, in_specs=in_specs, out_specs=(P('dp', None), cache_spec, cache_spec), check_vma=False)
```

time: 416 us -> 156 us (0.38)
  waiting for transfers between devices: 262 us -> 0 us
  Pallas kernels: 0 us -> 143 us
  other arithmetic: 86.9 us -> 0 us
  matrix products: 44.8 us -> 0 us
  between operations: 14.6 us -> 0.94 us
  local copies, waits for them, and re-layouts: 5.43 us -> 12.3 us
    psum x6 -> x0, waiting for transfers between devices: 261 us -> none  [tp_sum(): return lax.psum(part_out.astype(jnp.bfloat16), 'tp')]
    pallas_call x0 -> x4, Pallas kernels: none -> 143 us  [the longest x2 77.3 us: cross_and_mlp(): pl.pallas_call(functools.partial(cross_kernel, layer, tp, group), out_sha...]
    dot_general x22 -> x0, matrix products: 44.8 us -> none  [the longest x2 10.2 us: decoder_layer(): jnp.einsum('bhd,bshd->bhs', query_heads, cache_k, preferred_element_type=...]
    select_n x2 -> x0, other arithmetic: 35 us -> none  [the longest x1 24.7 us: decoder_layer(): cache_k = jnp.where(slot_hit, new_key, cache_k)]
    unnamed x2 -> x0, other arithmetic: 17.4 us -> none
    another operation x1 -> x0, other arithmetic: 17.4 us -> none  [local_step(): return (hidden, jnp.stack(keys_out), jnp.stack(vals_out))]
    reduce_sum x16 -> x0, other arithmetic: 9.73 us -> none  [the longest x6 6.3 us: layer_norm(): center = wide_vals - jnp.mean(wide_vals, axis=-1, keepdims=True)]
    unnamed x42 -> x55, local copies, waits for them, and re-layouts: 4.38 us -> 12.3 us
  transfers between devices with their start and end apart: 6 -> 0, of which waited for: 6 -> 0; matrix products, arithmetic and copies ran while one was open for 11% -> 0% of each run, Pallas kernels for 0% -> 0%
where the time goes in v1:
time: 156 us
  Pallas kernels  143 us (92%)
  local copies, waits for them, and re-layouts  12.3 us (8%)
    pallas_call x2, Pallas kernels, cross_and_mlp(): pl.pallas_call(functools.partial(cross_kernel, layer, tp, group), out_sha...  77.3 us
    pallas_call x2, Pallas kernels, self_attention(): pl.pallas_call(functools.partial(self_kernel, layer, group), out_shape=(j...  65.5 us
    unnamed x55, local copies, waits for them, and re-layouts  12.3 us

profile of v1, /device:TPU:113, one launch (start us, length us, event | category | flops | bytes accessed | tf_op | source)
XLA Modules:
  0.0 156.0 jit_solution(7165520854159414088)
XLA Ops:
  0.6 0.0 copy-start.4
  0.6 0.9 copy-done.4
  1.6 0.9 copy-done.6
  2.5 0.9 copy-done.8
  3.4 0.9 copy-done.10
  4.3 0.7 copy-done.15
  5.0 0.7 copy-done.17
  5.7 0.7 copy-done.22
  6.3 0.7 copy-done.25
  7.0 0.7 copy-done.26
  7.7 0.0 copy-start.12
  7.7 0.0 copy-start.13
  7.7 0.0 copy-start.14
  7.7 0.0 copy-start.16
  7.8 32.9 %self_attention.2 = (bf16[160,64]{1,0:T(8,128)(2,1)S(1)}, bf16[20480,448]{1,0:T(8,128)(2,1)}, bf16[20480,448]{1,0:T(8,128)(2,1)}) custom-call(s32[160]{0:T(256)S(1)} %copy-done.22, bf16[160,512]{1,0:T(8,128)(2,1)S(1)} %copy-done.4, bf16[3,2,512]{2,1,0:T(2,128)(2,1)S(1)} %bitcast.38, bf16[3,2,512]{2,1,0:T(2,128)(2,1)S(1)} %bitcast.42, ...), custom_call_target="tpu_custom_call" | custom-call | tf_op jit(solution)/shard_map/self_attention/pallas_call | solution.py:152
  40.6 0.0 copy-start.7
  40.6 0.0 copy-start.9
  40.7 0.0 copy-start.11
  40.8 40.0 %cross_and_mlp.2.hidden_ref = bf16[160,512]{1,0:T(8,128)(2,1)S(1)} custom-call(bf16[160,64]{1,0:T(8,128)(2,1)S(1)} %get-tuple-element.9.o_ref, bf16[160,512]{1,0:T(8,128)(2,1)S(1)} %copy-done.5, bf16[3,2,512]{2,1,0:T(2,128)(2,1)S(1)} %bitcast.39, bf16[3,2,512]{2,1,0:T(2,128)(2,1)S(1)} %bitcast.43, bf16[2,64,512]{2,1,0:T(8,128)(2,1)S(1)} %copy-done.12, ...), custom_call_target="tpu_custom_call" | custom-call | tf_op jit(solution)/shard_map/cross_and_mlp/pallas_call | solution.py:276
  80.9 32.6 %self_attention.3 = (bf16[160,64]{1,0:T(8,128)(2,1)S(1)}, bf16[20480,448]{1,0:T(8,128)(2,1)}, bf16[20480,448]{1,0:T(8,128)(2,1)}) custom-call(s32[160]{0:T(256)S(1)} %copy-done.22, bf16[160,512]{1,0:T(8,128)(2,1)S(1)} %cross_and_mlp.2.hidden_ref, bf16[3,2,512]{2,1,0:T(2,128)(2,1)S(1)} %bitcast.40, ...), custom_call_target="tpu_custom_call", output_to_operand_aliasing={{1}: (11, {}), {2}: (12, {})} | custom-call | tf_op jit(solution)/shard_map/self_attention/pallas_call | solution.py:152
  113.5 0.0 copy-start.1
  113.5 4.6 %copy-done.1 = bf16[2,32,1500,1,64]{2,4,3,1,0:T(8,128)(2,1)S(1)} copy-done((bf16[2,32,1500,1,64]{2,4,3,1,0:T(8,128)(2,1)S(1)}, bf16[2,32,1500,1,64]{2,4,3,1,0:T(8,128)(2,1)}, u32[]{:S(2)}) %copy-start.1) | copy-done | bytes 12288024
  118.1 37.2 %cross_and_mlp.3 = bf16[160,512]{1,0:T(8,128)(2,1)S(1)} custom-call(bf16[160,64]{1,0:T(8,128)(2,1)S(1)} %get-tuple-element.12.o_ref, bf16[160,512]{1,0:T(8,128)(2,1)S(1)} %cross_and_mlp.2.hidden_ref, bf16[3,2,512]{2,1,0:T(2,128)(2,1)S(1)} %bitcast.41, bf16[3,2,512]{2,1,0:T(2,128)(2,1)S(1)} %bitcast.45, bf16[2,64,512]{2,1,0:T(8,128)(2,1)S(1)} %copy-done.12, ...), custom_call_target="tpu_custom_call" | custom-call | tf_op jit(solution)/shard_map/cross_and_mlp/pallas_call | solution.py:276
  155.3 0.7 copy.33
  (35 shorter events, 0.1 us)
Async XLA Ops:
  0.6 0.9 copy-start.4
  1.6 0.9 copy-start.6
  2.5 0.9 copy-start.8
  3.4 0.9 copy-start.10
  4.3 0.7 copy-start.15
  5.0 0.7 copy-start.17
  7.6 33.0 %copy-start = (bf16[2,32,1500,1,64]{2,4,3,1,0:T(8,128)(2,1)S(1)}, bf16[2,32,1500,1,64]{2,4,3,1,0:T(8,128)(2,1)}, u32[]{:S(2)}) copy-start(bf16[2,32,1500,1,64]{2,4,3,1,0:T(8,128)(2,1)} %param.27) | copy-start | bytes 36864004
  7.6 33.0 %copy-start.2 = (bf16[2,512,256]{2,1,0:T(8,128)(2,1)S(1)}, bf16[2,512,256]{2,1,0:T(8,128)(2,1)}, u32[]{:S(2)}) copy-start(bf16[2,512,256]{2,1,0:T(8,128)(2,1)} %w1_ref.3) | copy-start | bytes 1572868
  7.6 33.0 %copy-start.3 = (bf16[2,256,512]{2,1,0:T(8,128)(2,1)S(1)}, bf16[2,256,512]{2,1,0:T(8,128)(2,1)}, u32[]{:S(2)}) copy-start(bf16[2,256,512]{2,1,0:T(8,128)(2,1)} %w2_ref.3) | copy-start | bytes 1572868
  7.7 33.1 %copy-start.5 = (bf16[160,512]{1,0:T(8,128)(2,1)S(1)}, bf16[160,512]{1,0:T(8,128)(2,1)}, u32[]{:S(2)}) copy-start(bf16[160,512]{1,0:T(8,128)(2,1)} %hidden_ref.3) | copy-start | bytes 491524
  7.7 33.1 %copy-start.12 = (bf16[2,64,512]{2,1,0:T(8,128)(2,1)S(1)}, bf16[2,64,512]{2,1,0:T(8,128)(2,1)}, u32[]{:S(2)}) copy-start(bf16[2,64,512]{2,1,0:T(8,128)(2,1)} %wo_ref.3) | copy-start | bytes 393220
  7.7 33.1 %copy-start.13 = (bf16[2,512,64]{1,2,0:T(8,128)(2,1)S(1)}, bf16[2,512,64]{1,2,0:T(8,128)(2,1)}, u32[]{:S(2)}) copy-start(bf16[2,512,64]{1,2,0:T(8,128)(2,1)} %param.38) | copy-start | bytes 393220
  7.7 33.1 %copy-start.14 = (bf16[2,64,512]{2,1,0:T(8,128)(2,1)S(1)}, bf16[2,64,512]{2,1,0:T(8,128)(2,1)}, u32[]{:S(2)}) copy-start(bf16[2,64,512]{2,1,0:T(8,128)(2,1)} %wco_ref.3) | copy-start | bytes 393220
  7.7 33.1 %copy-start.16 = (bf16[2,3,512]{2,0,1:T(2,128)(2,1)S(1)}, bf16[2,3,512]{2,0,1:T(2,128)(2,1)}, u32[]{:S(2)}) copy-start(bf16[2,3,512]{2,0,1:T(2,128)(2,1)} %param.29) | copy-start | bytes 18436
  7.7 33.1 %copy-start.18 = (bf16[2,3,512]{2,0,1:T(2,128)(2,1)S(1)}, bf16[2,3,512]{2,0,1:T(2,128)(2,1)}, u32[]{:S(2)}) copy-start(bf16[2,3,512]{2,0,1:T(2,128)(2,1)} %param.30) | copy-start | bytes 18436
  7.7 33.1 %copy-start.19 = (bf16[2,512]{1,0:T(2,128)(2,1)S(1)}, bf16[2,512]{1,0:T(2,128)(2,1)}, u32[]{:S(2)}) copy-start(bf16[2,512]{1,0:T(2,128)(2,1)} %bo_ref.3) | copy-start | bytes 6148
  7.7 33.1 %copy-start.20 = (bf16[2,512]{1,0:T(2,128)(2,1)S(1)}, bf16[2,512]{1,0:T(2,128)(2,1)}, u32[]{:S(2)}) copy-start(bf16[2,512]{1,0:T(2,128)(2,1)} %bco_ref.3) | copy-start | bytes 6148
  7.7 33.1 %copy-start.21 = (bf16[2,512]{1,0:T(2,128)(2,1)S(1)}, bf16[2,512]{1,0:T(2,128)(2,1)}, u32[]{:S(2)}) copy-start(bf16[2,512]{1,0:T(2,128)(2,1)} %b2_ref.3) | copy-start | bytes 6148
  7.7 33.1 %copy-start.23 = (bf16[2,256]{1,0:T(2,128)(2,1)S(1)}, bf16[2,256]{1,0:T(2,128)(2,1)}, u32[]{:S(2)}) copy-start(bf16[2,256]{1,0:T(2,128)(2,1)} %b1_ref.3) | copy-start | bytes 3076
  7.7 33.1 %copy-start.24 = (bf16[2,64]{1,0:T(2,128)(2,1)S(1)}, bf16[2,64]{1,0:T(2,128)(2,1)}, u32[]{:S(2)}) copy-start(bf16[2,64]{1,0:T(2,128)(2,1)} %bcq_ref.3) | copy-start | bytes 772
  40.6 40.2 %copy-start.7 = (bf16[2,512,64]{1,2,0:T(8,128)(2,1)S(1)}, bf16[2,512,64]{1,2,0:T(8,128)(2,1)}, u32[]{:S(2)}) copy-start(bf16[2,512,64]{1,2,0:T(8,128)(2,1)} %param.31) | copy-start | bytes 393220
  40.6 40.2 %copy-start.9 = (bf16[2,512,64]{1,2,0:T(8,128)(2,1)S(1)}, bf16[2,512,64]{1,2,0:T(8,128)(2,1)}, u32[]{:S(2)}) copy-start(bf16[2,512,64]{1,2,0:T(8,128)(2,1)} %param.33) | copy-start | bytes 393220
  40.7 40.2 %copy-start.11 = (bf16[2,512,64]{1,2,0:T(8,128)(2,1)S(1)}, bf16[2,512,64]{1,2,0:T(8,128)(2,1)}, u32[]{:S(2)}) copy-start(bf16[2,512,64]{1,2,0:T(8,128)(2,1)} %param.34) | copy-start | bytes 393220
  113.5 4.6 %copy-start.1 = (bf16[2,32,1500,1,64]{2,4,3,1,0:T(8,128)(2,1)S(1)}, bf16[2,32,1500,1,64]{2,4,3,1,0:T(8,128)(2,1)}, u32[]{:S(2)}) copy-start(bf16[2,32,1500,1,64]{2,4,3,1,0:T(8,128)(2,1)} %param.27) | copy-start | bytes 36864004
  (3 other events, 2.0 us)

commit v2 on v1

--- a/solution.py
+++ b/solution.py
@@ -42,10 +42,17 @@
     return ref[idx].astype(F32)
 
 
-def self_kernel(layer, group, pos_ref, hidden_ref, gain_ref, bias_ref, wq_ref, bq_ref, wk_ref, wv_ref, bv_ref, kin_ref, vin_ref, *rest):
-    o_ref, kout_ref, vout_ref, kbuf, vbuf, qbd, kcol, vcol, osc, in_sem, out_sem = rest[-11:]
+def load_all(pairs, sem):
+    copies = [pltpu.make_async_copy(src, dst, sem.at[n]) for n, (src, dst) in enumerate(pairs)]
+    for copy in copies:
+        copy.start()
+    return copies
+
+
+def self_kernel(layer, group, pos_hbm, hidden_hbm, gain_hbm, bias_hbm, wq_hbm, bq_hbm, wk_hbm, wv_hbm, bv_hbm, kin_ref, vin_ref, *rest):
+    (o_ref, kout_ref, vout_ref, kbuf, vbuf, qbd, kcol, vcol, scores, osc, pos_ref, hidden_ref, gain_ref, bias_ref, wq_ref, bq_ref, wk_ref, wv_ref, bv_ref, in_sem, out_sem, param_sem) = rest[-22:]
     batch = hidden_ref.shape[0]
-    head = wq_ref.shape[1]
+    head = wq_ref.shape[0]
     slots = kbuf.shape[2]
     groups = batch // group
     span = group * head
@@ -58,19 +65,22 @@
     def out_copy(buf, dst, which, g):
         return pltpu.make_async_copy(buf.at[g], dst.at[pl.ds(base + g * span, span), :], out_sem.at[which, g])
 
+    copies = load_all([(hidden_hbm, hidden_ref), (gain_hbm, gain_ref), (bias_hbm, bias_ref), (wq_hbm.at[layer], wq_ref), (bq_hbm, bq_ref), (wk_hbm.at[layer], wk_ref), (wv_hbm.at[layer], wv_ref), (bv_hbm, bv_ref), (pos_hbm, pos_ref)], param_sem)
+
     def start(g, carry):
         in_copy(kin_ref, kbuf, 0, g).start()
         in_copy(vin_ref, vbuf, 1, g).start()
         return carry
 
     lax.fori_loop(0, groups, start, 0)
+    for copy in copies:
+        copy.wait()
 
     normed = layer_norm(hidden_ref[...].astype(F32), gain_ref[0, layer:layer + 1, :].astype(F32), bias_ref[0, layer:layer + 1, :].astype(F32))
-    q = ((dot_nt(normed, wq_ref[layer]) + bq_ref[layer:layer + 1, :].astype(F32)) * scale).astype(BF16)
-    k = (dot_nt(normed, wk_ref[layer]) * scale).astype(BF16)
-    v = (dot_nt(normed, wv_ref[layer]) + bv_ref[layer:layer + 1, :].astype(F32)).astype(BF16)
-    eye = stack_eye(span, head)
-    wide_q = dot(q, eye)
+    q = ((dot_nt(normed, wq_ref[...]) + bq_ref[layer:layer + 1, :].astype(F32)) * scale).astype(BF16)
+    k = (dot_nt(normed, wk_ref[...]) * scale).astype(BF16)
+    v = (dot_nt(normed, wv_ref[...]) + bv_ref[layer:layer + 1, :].astype(F32)).astype(BF16)
+    wide_q = dot(q, stack_eye(span, head))
     diag = iota((batch, span), 0) % group == iota((batch, span), 1) // head
     qbd[...] = jnp.where(diag, wide_q, 0.0)
     k_t = k.astype(F32).T
@@ -79,51 +89,70 @@
         kcol[g] = k_t[:, g * group:(g + 1) * group]
         vcol[g] = v_t[:, g * group:(g + 1) * group]
 
-    lane_ids = iota((group, slots), 1)
-    row_ids = iota((group, slots), 0)
-    odiag = iota((span, group), 0) // head == iota((span, group), 1)
     full_tiles = slots // 128
     tail = slots - full_tiles * 128
 
-    def attend(g, carry):
+    def rows_of(g):
+        return pl.ds(pl.multiple_of(g * group, group), group)
+
+    def update(g):
         in_copy(kin_ref, kbuf, 0, g).wait()
         in_copy(vin_ref, vbuf, 1, g).wait()
         kc = kcol[g]
         vc = vcol[g]
-        limit = jnp.zeros((group, slots), jnp.int32)
         for i in range(group):
             pos = pos_ref[g * group + i]
-            limit = jnp.where(row_ids == i, pos, limit)
-            tile = pos // 128
-            local = pos - tile * 128
             rows = slice(i * head, (i + 1) * head)
-
-            def put(cols, width):
-                hit = iota((head, width), 1) == local
+            first = pl.multiple_of(jnp.minimum(pos // 128, full_tiles - 1) * 128, 128)
+            places = [(pl.ds(first, 128), iota((head, 128), 1) + first == pos)]
+            if tail:
+                places.append((slice(full_tiles * 128, slots), iota((head, tail), 1) + full_tiles * 128 == pos))
+            for cols, hit in places:
                 for buf, col in ((kbuf, kc), (vbuf, vc)):
                     old = buf[g, rows, cols].astype(F32)
                     buf[g, rows, cols] = jnp.where(hit, col[:, i:i + 1], old).astype(BF16)
 
-            @pl.when(tile < full_tiles)
-            def _():
-                put(pl.ds(pl.multiple_of(tile * 128, 128), 128), 128)
-
-            @pl.when(tile >= full_tiles)
-            def _():
-                put(slice(full_tiles * 128, slots), tail)
-
+    def score(g):
+        limit = jnp.zeros((group, 1), jnp.int32)
+        for i in range(group):
+            limit = jnp.where(iota((group, 1), 0) == i, pos_ref[g * group + i], limit)
+        raw = dot(qbd[rows_of(g), :].astype(BF16), kbuf[g])
+        scores[rows_of(g), :] = jnp.where(iota((group, slots), 1) <= limit, raw, NEG)
+
+    def write_back(g):
         out_copy(kbuf, kout_ref, 0, g).start()
         out_copy(vbuf, vout_ref, 1, g).start()
-        scores = dot(qbd[pl.ds(pl.multiple_of(g * group, group), group), :].astype(BF16), kbuf[g])
-        scores = jnp.where(lane_ids <= limit, scores, NEG)
-        probs = jnp.exp(scores - jnp.max(scores, axis=-1, keepdims=True))
-        probs = (probs / jnp.sum(probs, axis=-1, keepdims=True)).astype(BF16)
-        wide_o = dot_nt(vbuf[g], probs)
-        o_t = dot(eye, jnp.where(odiag, wide_o, 0.0).astype(BF16))
-        osc[pl.ds(pl.multiple_of(g * group, group), group), :] = o_t.T
+
+    def scan_keys(g, carry):
+        score(g - 1)
+        write_back(g - 1)
+        update(g)
         return carry
 
-    lax.fori_loop(0, groups, attend, 0)
+    update(0)
+    lax.fori_loop(1, groups, scan_keys, 0)
+    score(groups - 1)
+    write_back(groups - 1)
+
+    raw = scores[...]
+    probs = jnp.exp(raw - jnp.max(raw, axis=-1, keepdims=True))
+    scores[...] = probs * (1.0 / jnp.sum(probs, axis=-1, keepdims=True))
+
+    def weigh(g):
+        wide_o = dot_nt(vbuf[g], scores[rows_of(g), :].astype(BF16))
+        o_t = jnp.zeros((head, group), F32)
+        for i in range(group):
+            o_t = o_t + jnp.where(iota((head, group), 1) == i, wide_o[i * head:(i + 1) * head, :], 0.0)
+        osc[rows_of(g), :] = o_t.T
+
+    batch_of = 4
+
+    def scan_vals(n, carry):
+        for i in range(batch_of):
+            weigh(n * batch_of + i)
+        return carry
+
+    lax.fori_loop(0, groups // batch_of, scan_vals, 0)
     o_ref[...] = osc[...].astype(BF16)
 
     def finish(g, carry):
@@ -132,6 +161,10 @@
         return carry
 
     lax.fori_loop(0, groups, finish, 0)
+
+
+def in_hbm(arrays):
+    return [pltpu.with_memory_space_constraint(a, pltpu.HBM) for a in arrays]
 
 
 def self_attention(layer, hidden, positions, keys, vals, prev, params):
@@ -140,40 +173,48 @@
     slots = keys.shape[1]
     group = 8
     groups = batch // group
-    any_spec = pl.BlockSpec(memory_space=pltpu.HBM)
-    vm = pl.BlockSpec(memory_space=VMEM)
+    hbm = pl.BlockSpec(memory_space=pltpu.HBM)
     operands = [positions, hidden, params['ln_gain'], params['ln_bias'], params['w_query'], params['b_query'], params['w_key'], params['w_value'], params['b_value'], keys, vals]
-    in_specs = [pl.BlockSpec(memory_space=pltpu.SMEM)] + [vm] * 8 + [any_spec] * 2
     aliases = {}
     if prev is not None:
         operands += list(prev)
-        in_specs += [any_spec] * 2
         aliases = {11: 1, 12: 2}
+    weight = VMEM(params['w_query'].shape[1:], BF16)
+    vector = VMEM(params['b_query'].shape, BF16)
+    norm = VMEM(params['ln_gain'].shape, BF16)
     return pl.pallas_call(
         functools.partial(self_kernel, layer, group),
         out_shape=(jax.ShapeDtypeStruct((batch, head), BF16), jax.ShapeDtypeStruct(keys.shape, BF16), jax.ShapeDtypeStruct(vals.shape, BF16)),
-        in_specs=in_specs,
-        out_specs=(vm, any_spec, any_spec),
+        in_specs=[hbm] * len(operands),
+        out_specs=(pl.BlockSpec(memory_space=VMEM), hbm, hbm),
         scratch_shapes=[
             VMEM((groups, group * head, slots), BF16),
             VMEM((groups, group * head, slots), BF16),
             VMEM((batch, group * head), F32),
             VMEM((groups, head, group), F32),
             VMEM((groups, head, group), F32),
+            VMEM((batch, slots), F32),
             VMEM((batch, head), F32),
+            pltpu.SMEM((batch,), jnp.int32),
+            VMEM(hidden.shape, BF16),
+            norm, norm, weight, vector, weight, weight, vector,
             pltpu.SemaphoreType.DMA((2, groups)),
             pltpu.SemaphoreType.DMA((2, groups)),
+            pltpu.SemaphoreType.DMA((9,)),
         ],
         input_output_aliases=aliases,
         compiler_params=pltpu.CompilerParams(vmem_limit_bytes=40 * 2**20),
         name='self_attention',
-    )(*operands)
-
-
-def cross_kernel(layer, tp, group, o_ref, hidden_ref, gain_ref, bias_ref, wo_ref, bo_ref, wcq_ref, bcq_ref, wco_ref, bco_ref, w1_ref, b1_ref, w2_ref, b2_ref, kin_ref, vin_ref, hidden_out_ref, kbuf, vbuf, part, landed, blocks, qbd, osc, in_sem, rs_send, rs_recv, ag_send, ag_recv):
+    )(*in_hbm(operands))
+
+
+def cross_kernel(layer, tp, group, o_ref, hidden_hbm, *rest):
+    param_hbm, (kin_ref, vin_ref, hidden_out_ref, kbuf, vbuf, part, landed, blocks, qbd, scores, osc, hidden_ref), rest = rest[:12], rest[12:24], rest[24:]
+    param_refs, (param_sem, in_sem, rs_send, rs_recv, ag_send, ag_recv) = rest[:12], rest[12:]
+    gain_ref, bias_ref, bo_ref, bcq_ref, bco_ref, b1_ref, b2_ref, wo_ref, wcq_ref, wco_ref, w1_ref, w2_ref = param_refs
     me = lax.axis_index('tp')
     batch, width = hidden_ref.shape
-    head = wcq_ref.shape[1]
+    head = wcq_ref.shape[0]
     half = batch // 2
     quarters = width // 128
     chunks = kbuf.shape[0]
@@ -186,14 +227,22 @@
     def in_copy(src, buf, which, c):
         return pltpu.make_async_copy(src.at[pl.ds(base + c * span, span), :], buf.at[c], in_sem.at[which, c])
 
+    pairs = [(hidden_hbm, hidden_ref)]
+    for src, dst in zip(param_hbm, param_refs):
+        pairs.append((src if src.shape == dst.shape else src.at[layer], dst))
+    copies = load_all(pairs, param_sem)
     for c in range(chunks):
         in_copy(kin_ref, kbuf, 0, c).start()
+    for c in range(chunks):
         in_copy(vin_ref, vbuf, 1, c).start()
 
     barrier = pltpu.get_barrier_semaphore()
     peers = [lax.rem(me + step, tp) for step in range(1, tp)]
     for peer in peers:
         pl.semaphore_signal(barrier, inc=1, device_id={'tp': peer}, device_id_type=pl.DeviceIdType.MESH)
+
+    for copy in copies:
+        copy.wait()
 
     def bounds(j):
         r, c = j // quarters, j % quarters
@@ -237,29 +286,31 @@
         tops = [jnp.concatenate([blocks[x, r * quarters + c] for c in range(quarters)], axis=1) for r in range(tp // quarters)]
         return jnp.concatenate(tops, axis=0)
 
-    exchange(0, dot(o_ref[...], wo_ref[layer]), bo_ref, True)
+    exchange(0, dot(o_ref[...], wo_ref[...]), bo_ref, True)
 
     normed = layer_norm(whole(1).astype(F32), gain_ref[1, layer:layer + 1, :].astype(F32), bias_ref[1, layer:layer + 1, :].astype(F32))
-    q = ((dot_nt(normed, wcq_ref[layer]) + bcq_ref[layer:layer + 1, :].astype(F32)) * scale).astype(BF16)
-    eye = stack_eye(span, head)
+    q = ((dot_nt(normed, wcq_ref[...]) + bcq_ref[layer:layer + 1, :].astype(F32)) * scale).astype(BF16)
     diag = (iota((batch, span), 0) // beams) % group == iota((batch, span), 1) // head
-    qbd[...] = jnp.where(diag, dot(q, eye), 0.0)
-    odiag = iota((span, rows), 0) // head == iota((span, rows), 1) // beams
+    qbd[...] = jnp.where(diag, dot(q, stack_eye(span, head)), 0.0).astype(BF16)
     for c in range(chunks):
         in_copy(kin_ref, kbuf, 0, c).wait()
-        scores = dot(qbd[c * rows:(c + 1) * rows, :].astype(BF16), kbuf[c])
-        probs = jnp.exp(scores - jnp.max(scores, axis=-1, keepdims=True))
-        probs = (probs / jnp.sum(probs, axis=-1, keepdims=True)).astype(BF16)
+        scores[c * rows:(c + 1) * rows, :] = dot(qbd[c * rows:(c + 1) * rows, :], kbuf[c])
+    for c in range(chunks):
+        raw = scores[c * rows:(c + 1) * rows, :]
+        probs = jnp.exp(raw - jnp.max(raw, axis=-1, keepdims=True))
+        probs = (probs * (1.0 / jnp.sum(probs, axis=-1, keepdims=True))).astype(BF16)
         in_copy(vin_ref, vbuf, 1, c).wait()
         wide_o = dot_nt(vbuf[c], probs)
-        o_t = dot(eye, jnp.where(odiag, wide_o, 0.0).astype(BF16))
+        o_t = jnp.zeros((head, rows), F32)
+        for i in range(group):
+            o_t = o_t + jnp.where(iota((head, rows), 1) // beams == i, wide_o[i * head:(i + 1) * head, :], 0.0)
         osc[c * rows:(c + 1) * rows, :] = o_t.T
-    exchange(1, dot(osc[...].astype(BF16), wco_ref[layer]), bco_ref, False)
+    exchange(1, dot(osc[...].astype(BF16), wco_ref[...]), bco_ref, False)
 
     normed = layer_norm(whole(2).astype(F32), gain_ref[2, layer:layer + 1, :].astype(F32), bias_ref[2, layer:layer + 1, :].astype(F32))
-    inner = dot(normed, w1_ref[layer]) + b1_ref[layer:layer + 1, :].astype(F32)
+    inner = dot(normed, w1_ref[...]) + b1_ref[layer:layer + 1, :].astype(F32)
     inner = (0.5 * inner * (1.0 + lax.erf(inner * (0.5 ** 0.5)))).astype(BF16)
-    exchange(2, dot(inner, w2_ref[layer]), b2_ref, False)
+    exchange(2, dot(inner, w2_ref[...]), b2_ref, False)
     hidden_out_ref[...] = whole(3)
 
 
@@ -270,13 +321,15 @@
     group = 8
     chunks = audios // group
     vm = pl.BlockSpec(memory_space=VMEM)
-    any_spec = pl.BlockSpec(memory_space=pltpu.HBM)
-    names = ('ln_gain', 'ln_bias', 'w_out', 'b_out', 'w_cquery', 'b_cquery', 'w_cout', 'b_cout', 'w_fc1', 'b_fc1', 'w_fc2', 'b_fc2')
+    hbm = pl.BlockSpec(memory_space=pltpu.HBM)
+    vectors = ('ln_gain', 'ln_bias', 'b_out', 'b_cquery', 'b_cout', 'b_fc1', 'b_fc2')
+    weights = ('w_out', 'w_cquery', 'w_cout', 'w_fc1', 'w_fc2')
+    operands = [hidden] + [params[n] for n in vectors + weights] + [keys, vals]
     block = (batch // 2, 128)
     return pl.pallas_call(
         functools.partial(cross_kernel, layer, tp, group),
         out_shape=jax.ShapeDtypeStruct((batch, width), BF16),
-        in_specs=[vm] * 14 + [any_spec] * 2,
+        in_specs=[vm] + [hbm] * len(operands),
         out_specs=vm,
         scratch_shapes=[
             VMEM((chunks, group * head, frames), BF16),
@@ -284,8 +337,12 @@
             VMEM((3, tp) + block, BF16),
             VMEM((3, tp) + block, BF16),
             VMEM((4, tp) + block, BF16),
-            VMEM((batch, group * head), F32),
+            VMEM((batch, group * head), BF16),
+            VMEM((batch, frames), F32),
             VMEM((batch, head), F32),
+            VMEM(hidden.shape, BF16),
+        ] + [VMEM(params[n].shape, BF16) for n in vectors] + [VMEM(params[n].shape[1:], BF16) for n in weights] + [
+            pltpu.SemaphoreType.DMA((13,)),
             pltpu.SemaphoreType.DMA((2, chunks)),
             pltpu.SemaphoreType.DMA((3, tp - 1)),
             pltpu.SemaphoreType.DMA((3, tp)),
@@ -294,7 +351,7 @@
         ],
         compiler_params=pltpu.CompilerParams(vmem_limit_bytes=40 * 2**20, collective_id=layer, has_side_effects=True),
         name='cross_and_mlp',
-    )(attn_out, hidden, *[params[n] for n in names], keys, vals)
+    )(attn_out, *in_hbm(operands))
 
 
 def solution(mesh):

time: 156 us -> 118 us (0.76)
  Pallas kernels: 143 us -> 116 us
  local copies, waits for them, and re-layouts: 12.3 us -> 1.33 us
    pallas_call x2, Pallas kernels: 65.5 us -> 37.9 us  [self_attention(): pl.pallas_call(functools.partial(self_kernel, layer, group), out_shape=(j...]
    unnamed x55 -> x3, local copies, waits for them, and re-layouts: 12.3 us -> 1.33 us
where the time goes in v2:
time: 118 us
  Pallas kernels  116 us (98%)
  local copies, waits for them, and re-layouts  1.33 us (1%)
    pallas_call x2, Pallas kernels, cross_and_mlp(): pl.pallas_call(functools.partial(cross_kernel, layer, tp, group), out_sha...  78.5 us
    pallas_call x2, Pallas kernels, self_attention(): pl.pallas_call(functools.partial(self_kernel, layer, group), out_shape=(j...  37.9 us

profile of v2, /device:TPU:113, one launch (start us, length us, event | category | flops | bytes accessed | tf_op | source)
XLA Modules:
  0.0 118.4 jit_solution(6500777176886044699)
XLA Ops:
  0.6 18.9 %self_attention.2 = (bf16[160,64]{1,0:T(8,128)(2,1)S(1)}, bf16[20480,448]{1,0:T(8,128)(2,1)}, bf16[20480,448]{1,0:T(8,128)(2,1)}) custom-call(s32[160]{0:T(256)} %pos_hbm.3, bf16[160,512]{1,0:T(8,128)(2,1)} %hidden_hbm.3, bf16[3,2,512]{2,1,0:T(2,128)(2,1)} %bitcast.46, bf16[3,2,512]{2,1,0:T(2,128)(2,1)} %bitcast.50, bf16[2,64,512]{2,1,0:T(8,128)(2,1)} %bitcast.38, ...), custom_call_target="tpu_custom_call" | custom-call | tf_op jit(solution)/shard_map/self_attention/pallas_call | solution.py:185
  19.5 40.2 %cross_and_mlp.2.hidden_hbm = bf16[160,512]{1,0:T(8,128)(2,1)S(1)} custom-call(bf16[160,64]{1,0:T(8,128)(2,1)S(1)} %get-tuple-element.9.o_ref, bf16[160,512]{1,0:T(8,128)(2,1)} %hidden_hbm.3, bf16[3,2,512]{2,1,0:T(2,128)(2,1)} %bitcast.47, bf16[3,2,512]{2,1,0:T(2,128)(2,1)} %bitcast.51, bf16[2,512]{1,0:T(2,128)(2,1)} %rest_2_.3, bf16[2,64]{1,0:T(2,128)(2,1)} %rest_3_.3, ...), custom_call_target="tpu_custom_call" | custom-call | tf_op jit(solution)/shard_map/cross_and_mlp/pallas_call | solution.py:329
  59.8 0.0 copy-start
  59.8 0.7 copy-done
  60.4 19.1 %self_attention.3 = (bf16[160,64]{1,0:T(8,128)(2,1)S(1)}, bf16[20480,448]{1,0:T(8,128)(2,1)}, bf16[20480,448]{1,0:T(8,128)(2,1)}) custom-call(s32[160]{0:T(256)} %pos_hbm.3, bf16[160,512]{1,0:T(8,128)(2,1)} %copy-done, bf16[3,2,512]{2,1,0:T(2,128)(2,1)} %bitcast.48, bf16[3,2,512]{2,1,0:T(2,128)(2,1)} %bitcast.52, ...), custom_call_target="tpu_custom_call", output_to_operand_aliasing={{1}: (11, {}), {2}: (12, {})} | custom-call | tf_op jit(solution)/shard_map/self_attention/pallas_call | solution.py:185
  79.5 38.3 %cross_and_mlp.3 = bf16[160,512]{1,0:T(8,128)(2,1)S(1)} custom-call(bf16[160,64]{1,0:T(8,128)(2,1)S(1)} %get-tuple-element.12.o_ref, bf16[160,512]{1,0:T(8,128)(2,1)} %copy-done, bf16[3,2,512]{2,1,0:T(2,128)(2,1)} %bitcast.49, bf16[3,2,512]{2,1,0:T(2,128)(2,1)} %bitcast.53, bf16[2,512]{1,0:T(2,128)(2,1)} %rest_2_.3, bf16[2,64]{1,0:T(2,128)(2,1)} %rest_3_.3, ...), custom_call_target="tpu_custom_call" | custom-call | tf_op jit(solution)/shard_map/cross_and_mlp/pallas_call | solution.py:329
  117.7 0.7 copy.33
Async XLA Ops:
  59.8 0.7 copy-start

commit v3 on v2

v3 whole, which is shorter than its diff:
```python
import functools

import jax
import jax.numpy as jnp
from jax import lax
from jax.experimental import pallas as pl
from jax.experimental.pallas import tpu as pltpu
from jax.sharding import PartitionSpec as P

EPS = 1e-5
NEG = -1e30
PARAM_NAMES = ('ln_gain', 'ln_bias', 'w_query', 'b_query', 'w_key', 'w_value', 'b_value', 'w_out', 'b_out', 'w_cquery', 'b_cquery', 'w_cout', 'b_cout', 'w_fc1', 'b_fc1', 'w_fc2', 'b_fc2')
F32 = jnp.float32
BF16 = jnp.bfloat16
VMEM = pltpu.VMEM
NT = (((1,), (1,)), ((), ()))


def dot(a, b):
    return jnp.dot(a, b, preferred_element_type=F32)


def dot_nt(a, b):
    return lax.dot_general(a, b, NT, preferred_element_type=F32)


def layer_norm(wide_vals, gain_row, bias_row):
    center = wide_vals - jnp.mean(wide_vals, axis=-1, keepdims=True)
    var_est = jnp.mean(center * center, axis=-1, keepdims=True)
    return (center * lax.rsqrt(var_est + EPS) * gain_row + bias_row).astype(BF16)


def iota(shape, dim):
    return lax.broadcasted_iota(jnp.int32, shape, dim)


def stack_eye(rows, width):
    return (iota((width, rows), 1) % width == iota((width, rows), 0)).astype(BF16)


def row(ref, *idx):
    return ref[idx].astype(F32)


def load_all(pairs, sem):
    copies = [pltpu.make_async_copy(src, dst, sem.at[n]) for n, (src, dst) in enumerate(pairs)]
    for copy in copies:
        copy.start()
    return copies


def pack_half(vals):
    half = vals.shape[0] // 2
    return jnp.concatenate([vals[:half], vals[half:]], axis=1).astype(BF16)


def self_kernel(layer, group, streams, fetched, *refs):
    pos_hbm, hidden_in, gain_hbm, bias_hbm, wq_hbm, bq_hbm, wk_hbm, wv_hbm, bv_hbm, kin_ref, vin_ref = refs[:11]
    if fetched:
        o_ref, kout_ref, vout_ref, kbuf, vbuf = refs[13:18]
        hidden_ref = hidden_in
        rest = refs[18:]
    else:
        o_ref, kout_ref, vout_ref, kbuf, vbuf, hidden_ref = refs[11:17]
        rest = refs[17:]
    qbd, kcol, vcol, scores, osc, pos_ref, gain_ref, bias_ref, wq_ref, bq_ref, wk_ref, wv_ref, bv_ref, in_sem, out_sem, param_sem = rest
    batch = hidden_ref.shape[0]
    head = wq_ref.shape[0]
    slots = kbuf.shape[2]
    groups = batch // group
    span = group * head
    base = layer * batch * head
    scale = head ** -0.25

    def in_copy(src, buf, which, g):
        return pltpu.make_async_copy(src.at[pl.ds(base + g * span, span), :], buf.at[g], in_sem.at[which, g])

    def out_copy(buf, dst, which, g):
        return pltpu.make_async_copy(buf.at[g], dst.at[pl.ds(base + g * span, span), :], out_sem.at[which, g])

    pairs = [(gain_hbm, gain_ref), (bias_hbm, bias_ref), (wq_hbm.at[layer], wq_ref), (bq_hbm, bq_ref), (wk_hbm.at[layer], wk_ref), (wv_hbm.at[layer], wv_ref), (bv_hbm, bv_ref), (pos_hbm, pos_ref)]
    if not fetched:
        pairs.append((hidden_in, hidden_ref))
    copies = load_all(pairs, param_sem)

    def start(g, carry):
        in_copy(kin_ref, kbuf, 0, g).start()
        in_copy(vin_ref, vbuf, 1, g).start()
        return carry

    if not fetched:
        lax.fori_loop(0, groups, start, 0)
    for copy in copies:
        copy.wait()

    normed = layer_norm(hidden_ref[...].astype(F32), gain_ref[0, layer:layer + 1, :].astype(F32), bias_ref[0, layer:layer + 1, :].astype(F32))
    q = ((dot_nt(normed, wq_ref[...]) + bq_ref[layer:layer + 1, :].astype(F32)) * scale).astype(BF16)
    k = (dot_nt(normed, wk_ref[...]) * scale).astype(BF16)
    v = (dot_nt(normed, wv_ref[...]) + bv_ref[layer:layer + 1, :].astype(F32)).astype(BF16)
    wide_q = dot(q, stack_eye(span, head))
    diag = iota((batch, span), 0) % group == iota((batch, span), 1) // head
    qbd[...] = jnp.where(diag, wide_q, 0.0)
    k_t = k.astype(F32).T
    v_t = v.astype(F32).T
    for g in range(groups):
        kcol[g] = k_t[:, g * group:(g + 1) * group]
        vcol[g] = v_t[:, g * group:(g + 1) * group]

    full_tiles = slots // 128
    tail = slots - full_tiles * 128

    def rows_of(g, count=1):
        return pl.ds(pl.multiple_of(g * group, group), count * group)

    def update(g):
        if not fetched:
            in_copy(kin_ref, kbuf, 0, g).wait()
            in_copy(vin_ref, vbuf, 1, g).wait()
        kc = kcol[g]
        vc = vcol[g]
        for i in range(group):
            pos = pos_ref[g * group + i]
            rows = slice(i * head, (i + 1) * head)
            first = pl.multiple_of(jnp.minimum(pos // 128, full_tiles - 1) * 128, 128)
            places = [(pl.ds(first, 128), iota((head, 128), 1) + first == pos)]
            if tail:
                places.append((slice(full_tiles * 128, slots), iota((head, tail), 1) + full_tiles * 128 == pos))
            for cols, hit in places:
                for buf, col in ((kbuf, kc), (vbuf, vc)):
                    old = buf[g, rows, cols].astype(F32)
                    buf[g, rows, cols] = jnp.where(hit, col[:, i:i + 1], old).astype(BF16)

    def score(g):
        limit = jnp.zeros((group, 1), jnp.int32)
        for i in range(group):
            limit = jnp.where(iota((group, 1), 0) == i, pos_ref[g * group + i], limit)
        raw = dot(qbd[rows_of(g), :].astype(BF16), kbuf[g])
        scores[rows_of(g), :] = jnp.where(iota((group, slots), 1) <= limit, raw, NEG)

    def weigh(g):
        wide_o = dot_nt(vbuf[g], scores[rows_of(g), :].astype(BF16))
        o_t = jnp.zeros((head, group), F32)
        for i in range(group):
            o_t = o_t + jnp.where(iota((head, group), 1) == i, wide_o[i * head:(i + 1) * head, :], 0.0)
        osc[rows_of(g), :] = o_t.T

    batch_of = 4

    def attend(n, carry):
        first = n * batch_of
        for i in range(batch_of):
            update(first + i)
        for i in range(batch_of):
            score(first + i)
        for i in range(batch_of):
            out_copy(kbuf, kout_ref, 0, first + i).start()
            out_copy(vbuf, vout_ref, 1, first + i).start()
        raw = scores[rows_of(first, batch_of), :]
        probs = jnp.exp(raw - jnp.max(raw, axis=-1, keepdims=True))
        scores[rows_of(first, batch_of), :] = probs * (1.0 / jnp.sum(probs, axis=-1, keepdims=True))
        for i in range(batch_of):
            weigh(first + i)
        return carry

    lax.fori_loop(0, groups // batch_of, attend, 0)
    part = batch // streams
    for s in range(streams):
        o_ref[s] = pack_half(osc[s * part:(s + 1) * part, :])

    def finish(g, carry):
        out_copy(kbuf, kout_ref, 0, g).wait()
        out_copy(vbuf, vout_ref, 1, g).wait()
        return carry

    lax.fori_loop(0, groups, finish, 0)


def in_hbm(arrays):
    return [pltpu.with_memory_space_constraint(a, pltpu.HBM) for a in arrays]


def in_vmem(arrays):
    return [pltpu.with_memory_space_constraint(a, VMEM) for a in arrays]


def self_attention(layer, group, streams, hidden, positions, keys, vals, outs, params):
    fetched = outs is not None
    batch = hidden.shape[0]
    head = params['w_query'].shape[1]
    groups = batch // group
    vm = pl.BlockSpec(memory_space=VMEM)
    hbm = pl.BlockSpec(memory_space=pltpu.HBM)
    small = in_hbm([params[n] for n in ('ln_gain', 'ln_bias', 'w_query', 'b_query', 'w_key', 'w_value', 'b_value')])
    weight = VMEM(params['w_query'].shape[1:], BF16)
    vector = VMEM(params['b_query'].shape, BF16)
    norm = VMEM(params['ln_gain'].shape, BF16)
    if fetched:
        operands = in_hbm([positions]) + in_vmem([hidden]) + small + in_vmem([keys, vals]) + in_hbm(outs)
        in_specs = [hbm, vm] + [hbm] * 7 + [vm] * 2 + [hbm] * 2
        caches = list(outs)
        aliases = {9: 3, 10: 4, 11: 1, 12: 2}
        slots = keys.shape[2]
        extra_out = tuple(VMEM(a.shape, BF16) for a in (keys, vals))
        bufs = []
    else:
        operands = in_hbm([positions, hidden]) + small + in_hbm([keys, vals])
        in_specs = [hbm] * 11
        caches = [keys, vals]
        aliases = {}
        slots = keys.shape[1]
        extra_out = ()
        bufs = [VMEM((groups, group * head, slots), BF16)] * 2 + [VMEM(hidden.shape, BF16)]
    return pl.pallas_call(
        functools.partial(self_kernel, layer, group, streams, fetched),
        out_shape=(jax.ShapeDtypeStruct((streams, batch // streams // 2, 2 * head), BF16),) + tuple(jax.ShapeDtypeStruct(c.shape, BF16) for c in caches) + extra_out,
        in_specs=in_specs,
        out_specs=(vm, hbm, hbm) + (vm,) * len(extra_out),
        scratch_shapes=bufs + [
            VMEM((batch, group * head), F32),
            VMEM((groups, head, group), F32),
            VMEM((groups, head, group), F32),
            VMEM((batch, slots), F32),
            VMEM((batch, head), F32),
            pltpu.SMEM((batch,), jnp.int32),
            norm, norm, weight, vector, weight, weight, vector,
            pltpu.SemaphoreType.DMA((2, groups)),
            pltpu.SemaphoreType.DMA((2, groups)),
            pltpu.SemaphoreType.DMA((9,)),
        ],
        input_output_aliases=aliases,
        compiler_params=pltpu.CompilerParams(vmem_limit_bytes=(12 if fetched else 32) * 2**20),
        name='self_attention',
    )(*operands)[:3]


def cross_kernel(layer, layers, tp, group, streams, *refs):
    first, last = layer == 0, layer + 1 == layers
    refs = list(refs)
    o_ref, hidden_ref = refs[:2]
    param_hbm = refs[2:14]
    kin_ref, vin_ref = refs[14:16]
    del refs[:16]
    wo_in = None if first else refs.pop(0)
    if not last:
        wo_next_hbm, kself_ref, vself_ref = refs[:3]
        del refs[:3]
    hidden_out_ref = refs.pop(0)
    if not last:
        wo_out, kself_out, vself_out = refs[:3]
        del refs[:3]
    param_refs = refs[:12]
    gain_ref, bias_ref, bo_ref, bcq_ref, bco_ref, b1_ref, b2_ref, wo_ref, wcq_ref, wco_ref, w1_ref, w2_ref = param_refs
    (wo_next, kbuf, vbuf, part, landed, blocks, gathered, packed, wide_w, qbd, scores, param_sem, in_sem, self_sem, rs_send, rs_recv, ag_send, ag_recv, g_send, g_recv, w_send, w_recv) = refs[12:]
    me = lax.axis_index('tp')
    batch, width = hidden_ref.shape
    head = wcq_ref.shape[0]
    size = batch // streams
    half = size // 2
    quarters = width // 128
    chunks = kbuf.shape[0]
    span = kbuf.shape[1]
    base = layer * chunks * span
    scale = head ** -0.25
    beams = batch // (chunks * group)
    rows = group * beams
    per_stream = chunks // streams
    peers = [lax.rem(me + step, tp) for step in range(1, tp)]
    same_core = [lax.rem(me + step, tp) for step in range(2, tp, 2)]
    sibling = me + 1 - 2 * lax.rem(me, 2)

    def in_copy(src, buf, which, c):
        return pltpu.make_async_copy(src.at[pl.ds(base + c * span, span), :], buf.at[c], in_sem.at[which, c])

    def remote(src, dst, send_sem, recv_sem, peer):
        return pltpu.make_async_remote_copy(src, dst, send_sem, recv_sem, device_id={'tp': peer}, device_id_type=pl.DeviceIdType.MESH)

    barrier = pltpu.get_barrier_semaphore()
    for peer in peers:
        pl.semaphore_signal(barrier, inc=1, device_id={'tp': peer}, device_id_type=pl.DeviceIdType.MESH)

    pairs = [(src if src.shape == dst.shape else src.at[layer], dst) for src, dst in zip(param_hbm, param_refs)]
    if not last:
        pairs.append((wo_next_hbm.at[layer + 1], wo_next))
    copies = load_all(pairs, param_sem)
    for c in range(chunks):
        in_copy(kin_ref, kbuf, 0, c).start()
        in_copy(vin_ref, vbuf, 1, c).start()
    self_copies = []
    if not last:
        count, rows_self = kself_out.shape[:2]
        start_row = (layer + 1) * count * rows_self

        def self_copy(src, dst, which, g):
            return pltpu.make_async_copy(src.at[pl.ds(start_row + g * rows_self, rows_self), :], dst.at[g], self_sem.at[which, g])

        def start_self(g, carry):
            self_copy(kself_ref, kself_out, 0, g).start()
            self_copy(vself_ref, vself_out, 1, g).start()
            return carry

        def wait_self(g, carry):
            self_copy(kself_ref, kself_out, 0, g).wait()
            self_copy(vself_ref, vself_out, 1, g).wait()
            return carry

        lax.fori_loop(0, count, start_self, 0)
    for copy in copies:
        copy.wait()

    sends = []

    def send(*args):
        copy = remote(*args)
        copy.start()
        sends.append(copy)

    def vec(ref):
        return ref[layer:layer + 1, :].astype(F32)

    def norm(x, k):
        return layer_norm(x, gain_ref[k, layer:layer + 1, :].astype(F32), bias_ref[k, layer:layer + 1, :].astype(F32))

    def bounds(j):
        r, c = j // quarters, j % quarters
        return slice(r * half, (r + 1) * half), slice(c * 128, (c + 1) * 128)

    def scatter(x, s, total, hidden):
        for j in range(tp):
            rs, cs = bounds(j)
            part[x, s, j] = total[rs, cs].astype(BF16)
            blocks[x, s, j] = hidden[rs, cs].astype(BF16)
        for n, peer in enumerate(peers):
            send(part.at[x, s, peer], landed.at[x, s, me], rs_send.at[x, s, n], rs_recv.at[x, s, me], peer)

    def reduce_and_gather(x, s, bias_ref):
        bias = vec(bias_ref)
        own = lax.rem(me, quarters)
        bias_row = jnp.zeros((1, 128), F32)
        for c in range(quarters):
            bias_row = jnp.where(own == c, bias[:, c * 128:(c + 1) * 128], bias_row)
        acc = part[x, s, me].astype(F32) + blocks[x, s, me].astype(F32) + bias_row
        for n, peer in reversed(list(enumerate(peers))):
            remote(part.at[x, s, peer], landed.at[x, s, peer], rs_send.at[x, s, n], rs_recv.at[x, s, peer], peer).wait_recv()
            acc = acc + landed[x, s, peer].astype(F32)
        blocks[x, s, me] = acc.astype(BF16)
        for n, peer in enumerate(peers):
            send(blocks.at[x, s, me], blocks.at[x, s, me], ag_send.at[x, s, n], ag_recv.at[x, s, me], peer)

    def collect(x, s):
        for n, peer in enumerate(peers):
            remote(blocks.at[x, s, peer], blocks.at[x, s, peer], ag_send.at[x, s, n], ag_recv.at[x, s, peer], peer).wait_recv()
        return jnp.concatenate([jnp.concatenate([blocks[x, s, r * quarters + c].astype(F32) for c in range(quarters)], axis=1) for r in range(tp // quarters)], axis=0)

    def share(x, s, src):
        gathered[x, s, me] = src[s]
        for n, peer in enumerate(peers):
            send(src.at[s], gathered.at[x, s, me], g_send.at[x, s, n], g_recv.at[x, s, me], peer)

    def project_all(x, s, w_ref, bias_ref, hidden):
        for n, peer in enumerate(peers):
            remote(gathered.at[x, s, peer], gathered.at[x, s, peer], g_send.at[x, s, n], g_recv.at[x, s, peer], peer).wait_recv()
        vals = [gathered[x, s, j].astype(F32) for j in range(tp)]
        heads = jnp.concatenate([jnp.concatenate([v[:, :head] for v in vals], axis=1), jnp.concatenate([v[:, head:] for v in vals], axis=1)], axis=0)
        whole_w = w_ref[...].reshape(tp * head, width)
        return (hidden + dot(heads.astype(BF16), whole_w) + vec(bias_ref)).astype(BF16).astype(F32)

    def spread_weight(w, src):
        wide_w[w, me] = src[...]
        for n, peer in enumerate(same_core):
            send(src, wide_w.at[w, me], w_send.at[w, n], w_recv.at[w, me], peer)
        send(src, wide_w.at[w, me], w_send.at[w, tp // 2 - 1], w_recv.at[w, me], sibling)

    def forward_weight(w):
        for n, peer in enumerate(same_core):
            remote(wide_w.at[w, peer], wide_w.at[w, peer], w_send.at[w, n], w_recv.at[w, peer], peer).wait_recv()
            send(wide_w.at[w, peer], wide_w.at[w, peer], w_send.at[w, tp // 2 + n], w_recv.at[w, peer], sibling)

    def finish_weight(w):
        for step in range(0, tp, 2):
            origin = lax.rem(sibling + step, tp)
            remote(wide_w.at[w, origin], wide_w.at[w, origin], w_send.at[w, 0], w_recv.at[w, origin], sibling).wait_recv()

    def attend(s, hidden):
        q = ((dot_nt(norm(hidden, 1), wcq_ref[...]) + vec(bcq_ref)) * scale).astype(BF16)
        diag = (iota((size, span), 0) // beams) % group == iota((size, span), 1) // head
        qbd[s] = jnp.where(diag, dot(q, stack_eye(span, head)), 0.0).astype(BF16)
        for c in range(per_stream):
            in_copy(kin_ref, kbuf, 0, s * per_stream + c).wait()
            scores[s, c * rows:(c + 1) * rows, :] = dot(qbd[s, c * rows:(c + 1) * rows, :], kbuf[s * per_stream + c])
        outs = []
        for c in range(per_stream):
            raw = scores[s, c * rows:(c + 1) * rows, :]
            probs = jnp.exp(raw - jnp.max(raw, axis=-1, keepdims=True))
            probs = (probs * (1.0 / jnp.sum(probs, axis=-1, keepdims=True))).astype(BF16)
            in_copy(vin_ref, vbuf, 1, s * per_stream + c).wait()
            wide_o = dot_nt(vbuf[s * per_stream + c], probs)
            o_t = jnp.zeros((head, rows), F32)
            for i in range(group):
                o_t = o_t + jnp.where(iota((head, rows), 1) // beams == i, wide_o[i * head:(i + 1) * head, :], 0.0)
            outs.append(o_t.T)
        packed[s] = pack_half(jnp.concatenate(outs, axis=0))

    def mlp(hidden):
        inner = dot(norm(hidden, 2), w1_ref[...]) + vec(b1_ref)
        return dot((0.5 * inner * (1.0 + lax.erf(inner * (0.5 ** 0.5)))).astype(BF16), w2_ref[...])

    ids = range(streams)
    states = [hidden_ref[s * size:(s + 1) * size, :].astype(F32) for s in ids]
    if first:
        totals = []
        for s in ids:
            mine = o_ref[s].astype(F32)
            mine = jnp.concatenate([mine[:, :head], mine[:, head:]], axis=0).astype(BF16)
            totals.append(dot(mine, wo_ref[...]))
        pl.semaphore_wait(barrier, tp - 1)
        for s in ids:
            scatter(0, s, totals[s], states[s])
        for s in ids:
            reduce_and_gather(0, s, bo_ref)
        spread_weight(0, wco_ref)
        states = [None] * streams
    else:
        pl.semaphore_wait(barrier, tp - 1)
        for s in ids:
            share(0, s, o_ref)
        spread_weight(0, wco_ref)
    for s in ids:
        if first:
            states[s] = collect(0, s)
        else:
            states[s] = project_all(0, s, wo_in, bo_ref, states[s])
        attend(s, states[s])
        share(1, s, packed)
        if s == 0:
            forward_weight(0)
    if not last:
        spread_weight(1, wo_next)
    finish_weight(0)
    for s in ids:
        states[s] = project_all(1, s, wide_w.at[0], bco_ref, states[s])
        scatter(1, s, mlp(states[s]), states[s])
    for s in ids:
        reduce_and_gather(1, s, b2_ref)
    if not last:
        forward_weight(1)
    for s in ids:
        hidden_out_ref[s * size:(s + 1) * size, :] = collect(1, s).astype(BF16)
    if not last:
        finish_weight(1)
        wo_out[...] = wide_w[1]
        lax.fori_loop(0, count, wait_self, 0)
    for copy in sends:
        copy.wait_send()


def cross_and_mlp(layer, layers, tp, group, streams, attn_out, hidden, keys, vals, audios, params, wo_full, selfs, self_group):
    batch, width = hidden.shape
    head = params['w_cquery'].shape[1]
    frames = keys.shape[1]
    chunks = audios // group
    first, last = layer == 0, layer + 1 == layers
    vm = pl.BlockSpec(memory_space=VMEM)
    hbm = pl.BlockSpec(memory_space=pltpu.HBM)
    vectors = ('ln_gain', 'ln_bias', 'b_out', 'b_cquery', 'b_cout', 'b_fc1', 'b_fc2')
    weights = ('w_out', 'w_cquery', 'w_cout', 'w_fc1', 'w_fc2')
    operands = in_vmem([attn_out, hidden]) + in_hbm([params[n] for n in vectors + weights] + [keys, vals])
    in_specs = [vm] * 2 + [hbm] * 14
    out_shape = [VMEM((batch, width), BF16)]
    out_specs = [vm]
    wide = (tp,) + params['w_out'].shape[1:]
    if not first:
        operands += in_vmem([wo_full])
        in_specs += [vm]
    if not last:
        operands += in_hbm([params['w_out'], *selfs])
        in_specs += [hbm] * 3
        cache = (batch // self_group, self_group * head, selfs[0].shape[1])
        out_shape += [VMEM(wide, BF16), VMEM(cache, BF16), VMEM(cache, BF16)]
        out_specs += [vm] * 3
    block = (batch // streams // 2, 128)
    dma = pltpu.SemaphoreType.DMA
    return pl.pallas_call(
        functools.partial(cross_kernel, layer, layers, tp, group, streams),
        out_shape=tuple(out_shape),
        in_specs=in_specs,
        out_specs=tuple(out_specs),
        scratch_shapes=[VMEM(params[n].shape, BF16) for n in vectors] + [VMEM(params[n].shape[1:], BF16) for n in weights] + [
            VMEM(params['w_out'].shape[1:], BF16),
            VMEM((chunks, group * head, frames), BF16),
            VMEM((chunks, group * head, frames), BF16),
            VMEM((2, streams, tp) + block, BF16),
            VMEM((2, streams, tp) + block, BF16),
            VMEM((2, streams, tp) + block, BF16),
            VMEM((2, streams, tp) + block, BF16),
            VMEM((streams,) + block, BF16),
            VMEM((2,) + wide, BF16),
            VMEM((streams, batch // streams, group * head), BF16),
            VMEM((streams, batch // streams, frames), F32),
            dma((13,)),
            dma((2, chunks)),
            dma((2, batch // self_group)),
            dma((2, streams, tp - 1)),
            dma((2, streams, tp)),
            dma((2, streams, tp - 1)),
            dma((2, streams, tp)),
            dma((2, streams, tp - 1)),
            dma((2, streams, tp)),
            dma((2, tp)),
            dma((2, tp)),
        ],
        compiler_params=pltpu.CompilerParams(vmem_limit_bytes=24 * 2**20, collective_id=layer, has_side_effects=True),
        name='cross_and_mlp',
    )(*operands)


def solution(mesh):
    tp = mesh.shape['tp']
    cache_spec = P(None, 'dp', None, 'tp', None)
    col_spec = P(None, None, 'tp')
    row_spec = P(None, 'tp', None)
    vec_spec = P(None, 'tp')
    param_specs = {'ln_gain': P(), 'ln_bias': P(), 'w_query': col_spec, 'b_query': vec_spec, 'w_key': col_spec, 'w_value': col_spec, 'b_value': vec_spec, 'w_out': row_spec, 'b_out': P(), 'w_cquery': col_spec, 'b_cquery': vec_spec, 'w_cout': row_spec, 'b_cout': P(), 'w_fc1': col_spec, 'b_fc1': vec_spec, 'w_fc2': row_spec, 'b_fc2': P()}
    in_specs = (P('dp', None), P('dp'), cache_spec, cache_spec, cache_spec, cache_spec) + tuple(param_specs[param_name] for param_name in PARAM_NAMES)

    def flat(cache):
        layers, n, slots, heads, head = cache.shape
        return cache.transpose(0, 1, 3, 4, 2).reshape(layers * n * heads * head, slots)

    def local_step(hidden, positions, self_keys, self_vals, cross_keys, cross_vals, *layer_params):
        params = dict(zip(PARAM_NAMES, layer_params))
        for name in ('w_query', 'w_key', 'w_value', 'w_cquery'):
            params[name] = params[name].transpose(0, 2, 1)
        for name in ('ln_gain', 'ln_bias'):
            params[name] = params[name].transpose(1, 0, 2)
        layers, batch, slots, heads, head = self_keys.shape
        audios = cross_keys.shape[1]
        keys, vals, ckeys, cvals = flat(self_keys), flat(self_vals), flat(cross_keys), flat(cross_vals)
        streams, group, cross_group = 2, 8, 8
        outs, wo_full, keys_now, vals_now = None, None, keys, vals
        for layer in range(layers):
            attn_out, *outs = self_attention(layer, group, streams, hidden, positions, keys_now, vals_now, outs, params)
            hidden, *rest = cross_and_mlp(layer, layers, tp, cross_group, streams, attn_out, hidden, ckeys, cvals, audios, params, wo_full, (keys, vals), group)
            if rest:
                wo_full, keys_now, vals_now = rest

        def unflat(cache):
            return cache.reshape(layers, batch, heads, head, slots).transpose(0, 1, 4, 2, 3)

        return hidden, unflat(outs[0]), unflat(outs[1])

    return jax.shard_map(local_step, mesh=mesh, in_specs=in_specs, out_specs=(P('dp', None), cache_spec, cache_spec), check_vma=False)
```

time: 118 us -> 99.2 us (0.84)
  Pallas kernels: 116 us -> 97.6 us
    pallas_call x4, Pallas kernels: 116 us -> 97.6 us  [the longest x2 67.2 us: cross_and_mlp(): pl.pallas_call(functools.partial(cross_kernel, layer, layers, tp, group,...]
where the time goes in v3:
time: 99.2 us; the launch traced here: 99 us
  Pallas kernels  97.6 us (98%)
    pallas_call x2, Pallas kernels, cross_and_mlp(): pl.pallas_call(functools.partial(cross_kernel, layer, layers, tp, group,...  67.2 us
    pallas_call x2, Pallas kernels, self_attention(): pl.pallas_call(functools.partial(self_kernel, layer, group, streams, fetc...  30.4 us

profile of v3, /device:TPU:113, one launch (start us, length us, event | category | flops | bytes accessed | tf_op | source)
XLA Modules:
  0.0 99.0 jit_solution(2387955973672622685)
XLA Ops:
  0.6 0.0 copy-start
  0.6 15.9 %self_attention.2 = (bf16[2,40,128]{2,1,0:T(8,128)(2,1)S(1)}, bf16[20480,448]{1,0:T(8,128)(2,1)}, bf16[20480,448]{1,0:T(8,128)(2,1)}) custom-call(s32[160]{0:T(256)} %refs_0_.3, bf16[160,512]{1,0:T(8,128)(2,1)} %refs_1_.3, bf16[3,2,512]{2,1,0:T(2,128)(2,1)} %bitcast.46, bf16[3,2,512]{2,1,0:T(2,128)(2,1)} %bitcast.50, bf16[2,64,512]{2,1,0:T(8,128)(2,1)} %bitcast.38, ...), custom_call_target="tpu_custom_call" | custom-call | tf_op jit(solution)/shard_map/self_attention/pallas_call | solution.py:213
  16.5 0.0 copy-done
  16.5 36.8 %cross_and_mlp.2 = (bf16[160,512]{1,0:T(8,128)(2,1)S(1)}, bf16[8,64,512]{2,1,0:T(8,128)(2,1)S(1)}, bf16[20,512,448]{2,1,0:T(8,128)(2,1)S(1)}, bf16[20,512,448]{2,1,0:T(8,128)(2,1)S(1)}) custom-call(bf16[2,40,128]{2,1,0:T(8,128)(2,1)S(1)} %get-tuple-element.13.refs_0_, bf16[160,512]{1,0:T(8,128)(2,1)S(1)} %copy-done, bf16[3,2,512]{2,1,0:T(2,128)(2,1)} %bitcast.47, ...), custom_call_target="tpu_custom_call" | custom-call | tf_op jit(solution)/shard_map/cross_and_mlp/pallas_call | solution.py:482
  53.3 14.6 %self_attention.3 = (bf16[2,40,128]{2,1,0:T(8,128)(2,1)S(1)}, bf16[20480,448]{1,0:T(8,128)(2,1)}, bf16[20480,448]{1,0:T(8,128)(2,1)}, bf16[20,512,448]{2,1,0:T(8,128)(2,1)S(1)}, bf16[20,512,448]{2,1,0:T(8,128)(2,1)S(1)}) custom-call(s32[160]{0:T(256)} %refs_0_.3, ...), custom_call_target="tpu_custom_call", output_to_operand_aliasing={{3}: (9, {}), {4}: (10, {}), {1}: (11, {}), {2}: (12, {})} | custom-call | tf_op jit(solution)/shard_map/self_attention/pallas_call | solution.py:213
  67.9 30.4 %cross_and_mlp.3 = bf16[160,512]{1,0:T(8,128)(2,1)S(1)} custom-call(bf16[2,40,128]{2,1,0:T(8,128)(2,1)S(1)} %get-tuple-element.19.refs_0_, bf16[160,512]{1,0:T(8,128)(2,1)S(1)} %get-tuple-element.14.refs_1_, bf16[3,2,512]{2,1,0:T(2,128)(2,1)} %bitcast.49, bf16[3,2,512]{2,1,0:T(2,128)(2,1)} %bitcast.53, bf16[2,512]{1,0:T(2,128)(2,1)} %refs_4_.3, ...), custom_call_target="tpu_custom_call" | custom-call | tf_op jit(solution)/shard_map/cross_and_mlp/pallas_call | solution.py:482
  98.3 0.7 copy.37
Async XLA Ops:
  0.6 15.9 %copy-start = (bf16[160,512]{1,0:T(8,128)(2,1)S(1)}, bf16[160,512]{1,0:T(8,128)(2,1)}, u32[]{:S(2)}) copy-start(bf16[160,512]{1,0:T(8,128)(2,1)} %refs_1_.3) | copy-start | bytes 491524

commit v4 on v0

v4 whole, which is shorter than its diff:
```python
import functools

import jax
import jax.numpy as jnp
from jax import lax
from jax.experimental import pallas as pl
from jax.experimental.pallas import tpu as pltpu
from jax.sharding import PartitionSpec as P

EPS = 1e-5
NEG = -1e30
PARAM_NAMES = ('ln_gain', 'ln_bias', 'w_query', 'b_query', 'w_key', 'w_value', 'b_value', 'w_out', 'b_out', 'w_cquery', 'b_cquery', 'w_cout', 'b_cout', 'w_fc1', 'b_fc1', 'w_fc2', 'b_fc2')
F32 = jnp.float32
BF16 = jnp.bfloat16
VMEM = pltpu.VMEM
NT = (((1,), (1,)), ((), ()))


def dot(a, b):
    return jnp.dot(a, b, preferred_element_type=F32)


def dot_nt(a, b):
    return lax.dot_general(a, b, NT, preferred_element_type=F32)


def layer_norm(wide_vals, gain_row, bias_row):
    center = wide_vals - jnp.mean(wide_vals, axis=-1, keepdims=True)
    var_est = jnp.mean(center * center, axis=-1, keepdims=True)
    return (center * lax.rsqrt(var_est + EPS) * gain_row + bias_row).astype(BF16)


def repeat_lanes(vals, width):
    pair = jnp.concatenate([vals, vals], axis=1)
    return jnp.concatenate([pair] * (width // pair.shape[1]), axis=1)


def iota(shape, dim):
    return lax.broadcasted_iota(jnp.int32, shape, dim)


def load_all(pairs, sem):
    copies = [pltpu.make_async_copy(src, dst, sem.at[n]) for n, (src, dst) in enumerate(pairs)]
    for copy in copies:
        copy.start()
    return copies


def pack_half(vals):
    half = vals.shape[0] // 2
    return jnp.concatenate([vals[:half], vals[half:]], axis=1).astype(BF16)


def pack_half(vals):
    half = vals.shape[0] // 2
    return jnp.concatenate([vals[:half], vals[half:]], axis=1).astype(BF16)


def in_hbm(arrays):
    return [pltpu.with_memory_space_constraint(a, pltpu.HBM) for a in arrays]


def in_vmem(arrays):
    return [pltpu.with_memory_space_constraint(a, VMEM) for a in arrays]


VECTORS = ('ln_gain', 'ln_bias', 'b_query', 'b_value', 'b_out', 'b_cquery', 'b_cout', 'b_fc1', 'b_fc2')
WEIGHTS = ('w_query', 'w_key', 'w_value', 'w_out', 'w_cquery', 'w_cout', 'w_fc1', 'w_fc2')


def write_kernel(group, layers, pos_hbm, hidden_ref, knew_ref, vnew_ref, *refs):
    hidden_out_ref, kout_ref, vout_ref = refs[2 * layers:2 * layers + 3]
    kbufs = refs[2 * layers + 3:3 * layers + 3]
    vbufs = refs[3 * layers + 3:4 * layers + 3]
    kcol, vcol, pos_ref, pos_sem, hidden_sem, out_sem = refs[4 * layers + 3:]
    batch, head = knew_ref.shape[1:]
    groups, span, slots = kbufs[0].shape
    pos_copy = pltpu.make_async_copy(pos_hbm, pos_ref, pos_sem)
    pos_copy.start()
    hidden_copy = pltpu.make_async_copy(hidden_ref, hidden_out_ref, hidden_sem)
    hidden_copy.start()

    def out_copy(layer, which, g):
        buf, dst = ((kbufs[layer], kout_ref), (vbufs[layer], vout_ref))[which]
        return pltpu.make_async_copy(buf.at[g], dst.at[pl.ds((layer * groups + g) * span, span), :], out_sem.at[layer, which, g])

    full_tiles = slots // 128
    tail = slots - full_tiles * 128
    for layer in range(layers):
        k_t = knew_ref[layer].astype(F32).T
        v_t = vnew_ref[layer].astype(F32).T
        for g in range(groups):
            kcol[layer, g] = k_t[:, g * group:(g + 1) * group]
            vcol[layer, g] = v_t[:, g * group:(g + 1) * group]
    pos_copy.wait()

    for layer in range(layers):
        def update(g, carry):
            cols_of = (kcol[layer, g], vcol[layer, g])
            for i in range(group):
                pos = pos_ref[g * group + i]
                rows = slice(i * head, (i + 1) * head)
                first = pl.multiple_of(jnp.minimum(pos // 128, full_tiles - 1) * 128, 128)
                places = [(pl.ds(first, 128), iota((head, 128), 1) + first == pos)]
                if tail:
                    places.append((slice(full_tiles * 128, slots), iota((head, tail), 1) + full_tiles * 128 == pos))
                for cols, hit in places:
                    for buf, col in zip((kbufs[layer], vbufs[layer]), cols_of):
                        old = buf[g, rows, cols].astype(F32)
                        buf[g, rows, cols] = jnp.where(hit, col[:, i:i + 1], old).astype(BF16)
            out_copy(layer, 0, g).start()
            out_copy(layer, 1, g).start()
            return carry

        lax.fori_loop(0, groups, update, 0)

    for layer in range(layers):
        def finish(g, carry):
            out_copy(layer, 0, g).wait()
            out_copy(layer, 1, g).wait()
            return carry

        lax.fori_loop(0, groups, finish, 0)
    hidden_copy.wait()


def write_caches(group, positions, hidden, knew, vnew, kbufs, vbufs, flat_shape):
    layers, batch, head = knew.shape
    groups = kbufs[0].shape[0]
    vm = pl.BlockSpec(memory_space=VMEM)
    hbm = pl.BlockSpec(memory_space=pltpu.HBM)
    caches = list(kbufs) + list(vbufs)
    dma = pltpu.SemaphoreType.DMA
    return pl.pallas_call(
        functools.partial(write_kernel, group, layers),
        out_shape=(jax.ShapeDtypeStruct(hidden.shape, BF16),) + (jax.ShapeDtypeStruct(flat_shape, BF16),) * 2 + tuple(VMEM(c.shape, BF16) for c in caches),
        in_specs=[hbm] + [vm] * (3 + len(caches)),
        out_specs=(hbm, hbm, hbm) + (vm,) * len(caches),
        scratch_shapes=[
            VMEM((layers, groups, head, group), F32),
            VMEM((layers, groups, head, group), F32),
            pltpu.SMEM((batch,), jnp.int32),
            dma,
            dma,
            dma((layers, 2, groups)),
        ],
        input_output_aliases={4 + n: 3 + n for n in range(len(caches))},
        compiler_params=pltpu.CompilerParams(vmem_limit_bytes=43 * 2**19),
        name='write_caches',
    )(*in_hbm([positions]), *in_vmem([hidden, knew, vnew] + caches))[:3]


def layers_kernel(layers, tp, group, cross_group, streams, *refs):
    refs = list(refs)
    counts = (2, len(VECTORS), len(WEIGHTS), 4, 3, layers, layers, 2, len(VECTORS), len(WEIGHTS))
    split = []
    for count in counts:
        split.append(refs[:count])
        del refs[:count]
    (pos_hbm, hidden_hbm), vec_hbm, weight_hbm, (kself_ref, vself_ref, kin_ref, vin_ref), (hidden_out_ref, knew_ref, vnew_ref), kselfs, vselfs, (pos_ref, hidden_ref), vec_refs, weight_refs = split
    gain_ref, bias_ref, bq_ref, bv_ref, bo_ref, bcq_ref, bco_ref, b1_ref, b2_ref = vec_refs
    wq_ref, wk_ref, wv_ref, wo_ref, wcq_ref, wco_ref, w1_ref, w2_ref = weight_refs
    (kbuf, vbuf, part, landed, blocks, gathered, packed, wide_w, qself, sself, oself, qbd, scores, param_sem, self_sem, in_sem, rs_send, rs_recv, ag_send, ag_recv, g_send, g_recv, w_send, w_recv) = refs
    me = lax.axis_index('tp')
    batch, width = hidden_ref.shape
    head = wcq_ref.shape[1]
    size = batch // streams
    half = size // 2
    quarters = width // 128
    scale = head ** -0.25
    groups, span, slots = kselfs[0].shape
    chunks, cross_span = kbuf.shape[:2]
    beams = batch // (chunks * cross_group)
    rows = cross_group * beams
    per_stream = chunks // streams
    peers = [lax.rem(me + step, tp) for step in range(1, tp)]
    same_core = [lax.rem(me + step, tp) for step in range(2, tp, 2)]
    sibling = me + 1 - 2 * lax.rem(me, 2)
    ids = range(streams)

    def remote(src, dst, send_sem, recv_sem, peer):
        return pltpu.make_async_remote_copy(src, dst, send_sem, recv_sem, device_id={'tp': peer}, device_id_type=pl.DeviceIdType.MESH)

    barrier = pltpu.get_barrier_semaphore()
    for peer in peers:
        pl.semaphore_signal(barrier, inc=1, device_id={'tp': peer}, device_id_type=pl.DeviceIdType.MESH)

    copies = load_all(list(zip([pos_hbm, hidden_hbm] + vec_hbm + weight_hbm, [pos_ref, hidden_ref] + vec_refs + weight_refs)), param_sem)

    def self_copy(layer, which, g):
        src, dst = ((kself_ref, kselfs[layer]), (vself_ref, vselfs[layer]))[which]
        return pltpu.make_async_copy(src.at[pl.ds((layer * groups + g) * span, span), :], dst.at[g], self_sem.at[layer, which, g])

    def start_self(layer):
        def start(g, carry):
            self_copy(layer, 0, g).start()
            self_copy(layer, 1, g).start()
            return carry

        lax.fori_loop(0, groups, start, 0)

    def cross_copy(layer, which, c):
        src, buf = ((kin_ref, kbuf), (vin_ref, vbuf))[which]
        return pltpu.make_async_copy(src.at[pl.ds((layer * chunks + c) * cross_span, cross_span), :], buf.at[c], in_sem.at[layer, which, c])

    start_self(0)
    for copy in copies:
        copy.wait()
    sends = []

    def send(*args):
        copy = remote(*args)
        copy.start()
        sends.append(copy)

    def vec(ref, layer):
        return ref[layer:layer + 1, :].astype(F32)

    def norm(x, layer, k):
        return layer_norm(x, gain_ref[k, layer:layer + 1, :].astype(F32), bias_ref[k, layer:layer + 1, :].astype(F32))

    def bounds(j):
        r, c = j // quarters, j % quarters
        return slice(r * half, (r + 1) * half), slice(c * 128, (c + 1) * 128)

    def scatter(x, s, total, hidden):
        for j in range(tp):
            rs, cs = bounds(j)
            part[x, s, j] = total[rs, cs].astype(BF16)
            blocks[x, s, j] = hidden[rs, cs].astype(BF16)
        for n, peer in enumerate(peers):
            send(part.at[x, s, peer], landed.at[x, s, me], rs_send.at[x, s, n], rs_recv.at[x, s, me], peer)

    def reduce_and_gather(x, s, bias):
        own = lax.rem(me, quarters)
        bias_row = jnp.zeros((1, 128), F32)
        for c in range(quarters):
            bias_row = jnp.where(own == c, bias[:, c * 128:(c + 1) * 128], bias_row)
        for n, peer in reversed(list(enumerate(peers))):
            remote(part.at[x, s, peer], landed.at[x, s, peer], rs_send.at[x, s, n], rs_recv.at[x, s, peer], peer).wait_recv()
        acc = part[x, s, me].astype(F32) + blocks[x, s, me].astype(F32) + bias_row
        for peer in peers:
            acc = acc + landed[x, s, peer].astype(F32)
        blocks[x, s, me] = acc.astype(BF16)
        for n, peer in enumerate(peers):
            send(blocks.at[x, s, me], blocks.at[x, s, me], ag_send.at[x, s, n], ag_recv.at[x, s, me], peer)

    def collect(x, s):
        for n, peer in enumerate(peers):
            remote(blocks.at[x, s, peer], blocks.at[x, s, peer], ag_send.at[x, s, n], ag_recv.at[x, s, peer], peer).wait_recv()
        return jnp.concatenate([jnp.concatenate([blocks[x, s, r * quarters + c].astype(F32) for c in range(quarters)], axis=1) for r in range(tp // quarters)], axis=0)

    def share(x, s, vals):
        packed[x, s] = pack_half(vals)
        gathered[x, s, me] = packed[x, s]
        for n, peer in enumerate(peers):
            send(packed.at[x, s], gathered.at[x, s, me], g_send.at[x, s, n], g_recv.at[x, s, me], peer)

    def project_all(x, s, bias, hidden):
        for n, peer in enumerate(peers):
            remote(packed.at[x, s], gathered.at[x, s, peer], g_send.at[x, s, n], g_recv.at[x, s, peer], peer).wait_recv()
        vals = [gathered[x, s, j].astype(F32) for j in range(tp)]
        heads = jnp.concatenate([jnp.concatenate([v[:, :head] for v in vals], axis=1), jnp.concatenate([v[:, head:] for v in vals], axis=1)], axis=0)
        return (hidden + dot(heads.astype(BF16), wide_w[x].reshape(tp * head, width)) + bias).astype(BF16).astype(F32)

    def spread_weight(x):
        src = (wo_ref, wco_ref)[x % 2].at[x // 2]
        wide_w[x, me] = (wo_ref, wco_ref)[x % 2][x // 2]
        for n, peer in enumerate(same_core):
            send(src, wide_w.at[x, me], w_send.at[x, n], w_recv.at[x, me], peer)
        send(src, wide_w.at[x, me], w_send.at[x, tp // 2 - 1], w_recv.at[x, me], sibling)

    def forward_weight(x):
        for n, peer in enumerate(same_core):
            remote(wide_w.at[x, peer], wide_w.at[x, peer], w_send.at[x, n], w_recv.at[x, peer], peer).wait_recv()
            send(wide_w.at[x, peer], wide_w.at[x, peer], w_send.at[x, tp // 2 + n], w_recv.at[x, peer], sibling)

    def finish_weight(x):
        for step in range(0, tp, 2):
            origin = lax.rem(sibling + step, tp)
            remote(wide_w.at[x, origin], wide_w.at[x, origin], w_send.at[x, 0], w_recv.at[x, origin], sibling).wait_recv()

    self_batch = 5

    def self_attend(layer, s, hidden, after_projections):
        normed = norm(hidden, layer, 0)
        q = ((dot_nt(normed, wq_ref[layer]) + vec(bq_ref, layer)) * scale).astype(BF16)
        k = (dot_nt(normed, wk_ref[layer]) * scale).astype(BF16)
        v = (dot_nt(normed, wv_ref[layer]) + vec(bv_ref, layer)).astype(BF16)
        mine = slice(s * size, (s + 1) * size)
        knew_ref[layer, mine, :] = k
        vnew_ref[layer, mine, :] = v
        diag = iota((size, span), 0) % group == iota((size, span), 1) // head
        qself[...] = jnp.where(diag, repeat_lanes(q.astype(F32), span), 0.0)
        new_score = jnp.sum(q.astype(F32) * k.astype(F32), axis=-1, keepdims=True)
        after_projections()
        first_group = s * (size // group)

        count = size // group

        def score(g):
            limit = jnp.zeros((group, 1), jnp.int32)
            for i in range(group):
                limit = jnp.where(iota((group, 1), 0) == i, pos_ref[(first_group + g) * group + i], limit)
            raw = dot(qself[g * group:(g + 1) * group, :].astype(BF16), kselfs[layer][first_group + g])
            sself[g * group:(g + 1) * group, :] = jnp.where(iota((group, slots), 1) < limit, raw, NEG)

        def weigh(g):
            wide_o = dot_nt(vselfs[layer][first_group + g], sself[g * group:(g + 1) * group, :].astype(BF16))
            o_t = jnp.zeros((head, group), F32)
            for i in range(group):
                o_t = o_t + jnp.where(iota((head, group), 1) == i, wide_o[i * head:(i + 1) * head, :], 0.0)
            oself[g * group:(g + 1) * group, :] = o_t.T

        def batched(step, which):
            for n in range(0, count, self_batch):
                for g in range(n, n + self_batch):
                    self_copy(layer, which, first_group + g).wait()
                for g in range(n, n + self_batch):
                    step(g)

        batched(score, 0)
        raw = sself[...]
        top = jnp.maximum(jnp.max(raw, axis=-1, keepdims=True), new_score)
        probs = jnp.exp(raw - top)
        new_prob = jnp.exp(new_score - top)
        inv = 1.0 / (jnp.sum(probs, axis=-1, keepdims=True) + new_prob)
        sself[...] = probs * inv
        batched(weigh, 1)
        return oself[...] + (new_prob * inv).astype(BF16).astype(F32) * v.astype(F32)

    def cross_attend(layer, s, hidden):
        q = ((dot_nt(norm(hidden, layer, 1), wcq_ref[layer]) + vec(bcq_ref, layer)) * scale).astype(BF16)
        diag = (iota((size, cross_span), 0) // beams) % cross_group == iota((size, cross_span), 1) // head
        qbd[s] = jnp.where(diag, repeat_lanes(q.astype(F32), cross_span), 0.0).astype(BF16)
        for c in range(per_stream):
            cross_copy(layer, 0, s * per_stream + c).wait()
            cross_copy(layer, 1, s * per_stream + c).wait()
        for c in range(per_stream):
            scores[s, c * rows:(c + 1) * rows, :] = dot(qbd[s, c * rows:(c + 1) * rows, :], kbuf[s * per_stream + c])
        outs = []
        for c in range(per_stream):
            raw = scores[s, c * rows:(c + 1) * rows, :]
            probs = jnp.exp(raw - jnp.max(raw, axis=-1, keepdims=True))
            probs = (probs * (1.0 / jnp.sum(probs, axis=-1, keepdims=True))).astype(BF16)
            wide_o = dot_nt(vbuf[s * per_stream + c], probs)
            o_t = jnp.zeros((head, rows), F32)
            for i in range(cross_group):
                o_t = o_t + jnp.where(iota((head, rows), 1) // beams == i, wide_o[i * head:(i + 1) * head, :], 0.0)
            outs.append(o_t.T)
        return jnp.concatenate(outs, axis=0)

    def start_cross(layer, s):
        for c in range(s * per_stream, (s + 1) * per_stream):
            cross_copy(layer, 0, c).start()
            cross_copy(layer, 1, c).start()

    def mlp(layer, hidden):
        inner = dot(norm(hidden, layer, 2), w1_ref[layer]) + vec(b1_ref, layer)
        return dot((0.5 * inner * (1.0 + lax.erf(inner * (0.5 ** 0.5)))).astype(BF16), w2_ref[layer])

    def enter():
        pl.semaphore_wait(barrier, tp - 1)
        spread_weight(0)

    states = [hidden_ref[s * size:(s + 1) * size, :].astype(F32) for s in ids]
    for layer in range(layers):
        early, late = 2 * layer, 2 * layer + 1
        for s in ids:
            if layer:
                states[s] = collect(layer - 1, s)
            begin = layer == 0 and s == 0
            share(early, s, self_attend(layer, s, states[s], enter if begin else lambda: None))
            if layer == 0:
                start_cross(0, s)
        if layer == 0:
            spread_weight(late)
            forward_weight(early)
        if layer + 1 < layers:
            start_self(layer + 1)
        finish_weight(early)
        for s in ids:
            states[s] = project_all(early, s, vec(bo_ref, layer), states[s])
            share(late, s, cross_attend(layer, s, states[s]))
            if layer + 1 < layers:
                start_cross(layer + 1, s)
            if s == 0 and layer == 0:
                forward_weight(late)
        finish_weight(late)
        if layer + 1 < layers:
            spread_weight(early + 2)
            spread_weight(late + 2)
        for s in ids:
            states[s] = project_all(late, s, vec(bco_ref, layer), states[s])
            scatter(layer, s, mlp(layer, states[s]), states[s])
        for s in ids:
            reduce_and_gather(layer, s, vec(b2_ref, layer))
        if layer + 1 < layers:
            forward_weight(early + 2)
            forward_weight(late + 2)
    for s in ids:
        hidden_out_ref[s * size:(s + 1) * size, :] = collect(layers - 1, s).astype(BF16)
    for copy in sends:
        copy.wait_send()


def run_layers(tp, group, cross_group, streams, hidden, positions, keys, vals, ckeys, cvals, params):
    batch, width = hidden.shape
    layers, head = params['w_cquery'].shape[:2]
    slots, frames = keys.shape[1], ckeys.shape[1]
    chunks = ckeys.shape[0] // layers // head // cross_group
    groups = batch // group
    size = batch // streams
    vm = pl.BlockSpec(memory_space=VMEM)
    hbm = pl.BlockSpec(memory_space=pltpu.HBM)
    operands = [positions, hidden] + [params[n] for n in VECTORS + WEIGHTS] + [keys, vals, ckeys, cvals]
    cache = VMEM((groups, group * head, slots), BF16)
    fresh = VMEM((layers, batch, head), BF16)
    block = (size // 2, 128)
    dma = pltpu.SemaphoreType.DMA
    hidden_out, knew, vnew, *caches = pl.pallas_call(
        functools.partial(layers_kernel, layers, tp, group, cross_group, streams),
        out_shape=(VMEM(hidden.shape, BF16), fresh, fresh) + (cache,) * (2 * layers),
        in_specs=[hbm] * len(operands),
        out_specs=(vm,) * (3 + 2 * layers),
        scratch_shapes=[pltpu.SMEM((batch,), jnp.int32), VMEM(hidden.shape, BF16)] + [VMEM(params[n].shape, BF16) for n in VECTORS + WEIGHTS] + [
            VMEM((chunks, cross_group * head, frames), BF16),
            VMEM((chunks, cross_group * head, frames), BF16),
            VMEM((layers, streams, tp) + block, BF16),
            VMEM((layers, streams, tp) + block, BF16),
            VMEM((layers, streams, tp) + block, BF16),
            VMEM((2 * layers, streams, tp) + block, BF16),
            VMEM((2 * layers, streams) + block, BF16),
            VMEM((2 * layers, tp) + params['w_out'].shape[1:], BF16),
            VMEM((size, group * head), F32),
            VMEM((size, slots), F32),
            VMEM((size, head), F32),
            VMEM((streams, size, cross_group * head), BF16),
            VMEM((streams, size, frames), F32),
            dma((2 + len(VECTORS) + len(WEIGHTS),)),
            dma((layers, 2, groups)),
            dma((layers, 2, chunks)),
            dma((layers, streams, tp - 1)),
            dma((layers, streams, tp)),
            dma((layers, streams, tp - 1)),
            dma((layers, streams, tp)),
            dma((2 * layers, streams, tp - 1)),
            dma((2 * layers, streams, tp)),
            dma((2 * layers, tp)),
            dma((2 * layers, tp)),
        ],
        compiler_params=pltpu.CompilerParams(vmem_limit_bytes=43 * 2**19, collective_id=0, has_side_effects=True),
        name='decoder_layers',
    )(*in_hbm(operands))
    return hidden_out, knew, vnew, caches[:layers], caches[layers:]


def solution(mesh):
    tp = mesh.shape['tp']
    cache_spec = P(None, 'dp', None, 'tp', None)
    col_spec = P(None, None, 'tp')
    row_spec = P(None, 'tp', None)
    vec_spec = P(None, 'tp')
    param_specs = {'ln_gain': P(), 'ln_bias': P(), 'w_query': col_spec, 'b_query': vec_spec, 'w_key': col_spec, 'w_value': col_spec, 'b_value': vec_spec, 'w_out': row_spec, 'b_out': P(), 'w_cquery': col_spec, 'b_cquery': vec_spec, 'w_cout': row_spec, 'b_cout': P(), 'w_fc1': col_spec, 'b_fc1': vec_spec, 'w_fc2': row_spec, 'b_fc2': P()}
    in_specs = (P('dp', None), P('dp'), cache_spec, cache_spec, cache_spec, cache_spec) + tuple(param_specs[param_name] for param_name in PARAM_NAMES)

    def flat(cache):
        layers, n, slots, heads, head = cache.shape
        return cache.transpose(0, 1, 3, 4, 2).reshape(layers * n * heads * head, slots)

    def local_step(hidden, positions, self_keys, self_vals, cross_keys, cross_vals, *layer_params):
        params = dict(zip(PARAM_NAMES, layer_params))
        for name in ('w_query', 'w_key', 'w_value', 'w_cquery'):
            params[name] = params[name].transpose(0, 2, 1)
        for name in ('ln_gain', 'ln_bias'):
            params[name] = params[name].transpose(1, 0, 2)
        layers, batch, slots, heads, head = self_keys.shape
        keys, vals, ckeys, cvals = flat(self_keys), flat(self_vals), flat(cross_keys), flat(cross_vals)
        streams, group, cross_group = 2, 8, 8
        hidden, knew, vnew, kbufs, vbufs = run_layers(tp, group, cross_group, streams, hidden, positions, keys, vals, ckeys, cvals, params)
        hidden, *outs = write_caches(group, positions, hidden, knew, vnew, kbufs, vbufs, keys.shape)

        def unflat(cache):
            return cache.reshape(layers, batch, heads, head, slots).transpose(0, 1, 4, 2, 3)

        return hidden, unflat(outs[0]), unflat(outs[1])

    return jax.shard_map(local_step, mesh=mesh, in_specs=in_specs, out_specs=(P('dp', None), cache_spec, cache_spec), check_vma=False)
```

time: 416 us -> 81.7 us (0.20)
  waiting for transfers between devices: 262 us -> 0 us
  other arithmetic: 86.9 us -> 0 us
  Pallas kernels: 0 us -> 80.8 us
  matrix products: 44.8 us -> 0 us
  between operations: 14.6 us -> 0.81 us
  local copies, waits for them, and re-layouts: 5.43 us -> 0 us
    psum x6 -> x0, waiting for transfers between devices: 261 us -> none  [tp_sum(): return lax.psum(part_out.astype(jnp.bfloat16), 'tp')]
    pallas_call x0 -> x2, Pallas kernels: none -> 80.8 us  [the longest x1 65.8 us: run_layers(): pl.pallas_call(functools.partial(layers_kernel, layers, tp, group, cross_...]
    dot_general x22 -> x0, matrix products: 44.8 us -> none  [the longest x2 10.2 us: decoder_layer(): jnp.einsum('bhd,bshd->bhs', query_heads, cache_k, preferred_element_type=...]
    select_n x2 -> x0, other arithmetic: 35 us -> none  [the longest x1 24.7 us: decoder_layer(): cache_k = jnp.where(slot_hit, new_key, cache_k)]
    unnamed x2 -> x0, other arithmetic: 17.4 us -> none
    another operation x1 -> x0, other arithmetic: 17.4 us -> none  [local_step(): return (hidden, jnp.stack(keys_out), jnp.stack(vals_out))]
    reduce_sum x16 -> x0, other arithmetic: 9.73 us -> none  [the longest x6 6.3 us: layer_norm(): center = wide_vals - jnp.mean(wide_vals, axis=-1, keepdims=True)]
    convert_element_type x7 -> x0, other arithmetic: 4.74 us -> none  [the longest x1 1.63 us: decoder_layer(): (hidden.astype(jnp.float32) + mlp_sum + layer_w['b_fc2']).astype(jnp.bflo...]
  transfers between devices with their start and end apart: 6 -> 0, of which waited for: 6 -> 0; matrix products, arithmetic and copies ran while one was open for 11% -> 0% of each run, Pallas kernels for 0% -> 0%
where the time goes in v4:
time: 81.7 us; the launch traced here: 81.6 us
  Pallas kernels  80.8 us (99%)
    pallas_call x1, Pallas kernels, run_layers(): pl.pallas_call(functools.partial(layers_kernel, layers, tp, group, cross_...  65.8 us
    pallas_call x1, Pallas kernels, write_caches(): pl.pallas_call(functools.partial(write_kernel, group, layers), out_shape=...  15 us

profile of v4, /device:TPU:113, one launch (start us, length us, event | category | flops | bytes accessed | tf_op | source)
XLA Modules:
  0.0 81.6 jit_solution(1079912191741855954)
XLA Ops:
  0.6 65.8 %decoder_layers.1 = (bf16[160,512]{1,0:T(8,128)(2,1)S(1)}, bf16[2,160,64]{2,1,0:T(8,128)(2,1)S(1)}, bf16[2,160,64]{2,1,0:T(8,128)(2,1)S(1)}, bf16[20,512,448]{2,...) custom-call(s32[160]{0:T(256)} %pos_hbm.1, ...), custom_call_target="tpu_custom_call" | custom-call | tf_op jit(solution)/shard_map/decoder_layers/pallas_call | solution.py:421
  66.5 15.0 %write_caches.1 = (bf16[160,512]{1,0:T(8,128)(2,1)}, bf16[20480,448]{1,0:T(8,128)(2,1)}, bf16[20480,448]{1,0:T(8,128)(2,1)}, bf16[20,512,448]{2,1,0:T(8,128)(2,1...) custom-call(s32[160]{0:T(256)} %pos_hbm.1, ...), custom_call_target="tpu_custom_call", output_to_operand_aliasing={{3}: (4, {}), {4}: (5, {}), {5}: (6, {}), {6}: (7, {})} | custom-call | tf_op jit(solution)/shard_map/write_caches/pallas_call | solution.py:134

commit v5 on v4

--- a/solution.py
+++ b/solution.py
@@ -92,9 +92,9 @@
         for g in range(groups):
             kcol[layer, g] = k_t[:, g * group:(g + 1) * group]
             vcol[layer, g] = v_t[:, g * group:(g + 1) * group]
-    pos_copy.wait()
-
-    for layer in range(layers):
+        if layer == 0:
+            pos_copy.wait()
+
         def update(g, carry):
             cols_of = (kcol[layer, g], vcol[layer, g])
             for i in range(group):
@@ -173,8 +173,8 @@
     beams = batch // (chunks * cross_group)
     rows = cross_group * beams
     per_stream = chunks // streams
-    peers = [lax.rem(me + step, tp) for step in range(1, tp)]
-    same_core = [lax.rem(me + step, tp) for step in range(2, tp, 2)]
+    peers = [lax.rem(me + step, tp) for step in sorted(range(1, tp), key=lambda step: abs(step - tp // 2))]
+    same_core = [lax.rem(me + step, tp) for step in sorted(range(2, tp, 2), key=lambda step: abs(step - tp // 2))]
     sibling = me + 1 - 2 * lax.rem(me, 2)
     ids = range(streams)
 
@@ -185,25 +185,31 @@
     for peer in peers:
         pl.semaphore_signal(barrier, inc=1, device_id={'tp': peer}, device_id_type=pl.DeviceIdType.MESH)
 
-    copies = load_all(list(zip([pos_hbm, hidden_hbm] + vec_hbm + weight_hbm, [pos_ref, hidden_ref] + vec_refs + weight_refs)), param_sem)
+    pairs = list(zip([pos_hbm, hidden_hbm] + vec_hbm + weight_hbm, [pos_ref, hidden_ref] + vec_refs + weight_refs))
+    needed_first = 2 + len(vec_refs) + 3
+    copies = load_all(pairs[:needed_first], param_sem)
 
     def self_copy(layer, which, g):
         src, dst = ((kself_ref, kselfs[layer]), (vself_ref, vselfs[layer]))[which]
         return pltpu.make_async_copy(src.at[pl.ds((layer * groups + g) * span, span), :], dst.at[g], self_sem.at[layer, which, g])
 
-    def start_self(layer):
+    def start_self(layer, which, s):
         def start(g, carry):
-            self_copy(layer, 0, g).start()
-            self_copy(layer, 1, g).start()
+            self_copy(layer, which, g).start()
             return carry
 
-        lax.fori_loop(0, groups, start, 0)
+        lax.fori_loop(s * (size // group), (s + 1) * (size // group), start, 0)
 
     def cross_copy(layer, which, c):
         src, buf = ((kin_ref, kbuf), (vin_ref, vbuf))[which]
         return pltpu.make_async_copy(src.at[pl.ds((layer * chunks + c) * cross_span, cross_span), :], buf.at[c], in_sem.at[layer, which, c])
 
-    start_self(0)
+    late_copies = [pltpu.make_async_copy(src, dst, param_sem.at[needed_first + n]) for n, (src, dst) in enumerate(pairs[needed_first:])]
+    for copy in late_copies:
+        copy.start()
+    for s in ids:
+        start_self(0, 0, s)
+        start_self(0, 1, s)
     for copy in copies:
         copy.wait()
     sends = []
@@ -360,6 +366,8 @@
         return dot((0.5 * inner * (1.0 + lax.erf(inner * (0.5 ** 0.5)))).astype(BF16), w2_ref[layer])
 
     def enter():
+        for copy in late_copies:
+            copy.wait()
         pl.semaphore_wait(barrier, tp - 1)
         spread_weight(0)
 
@@ -373,31 +381,31 @@
             share(early, s, self_attend(layer, s, states[s], enter if begin else lambda: None))
             if layer == 0:
                 start_cross(0, s)
+            if s == 0:
+                spread_weight(late)
+                if layer:
+                    forward_weight(early)
         if layer == 0:
-            spread_weight(late)
             forward_weight(early)
         if layer + 1 < layers:
-            start_self(layer + 1)
+            for s in ids:
+                start_self(layer + 1, 0, s)
+                start_self(layer + 1, 1, s)
         finish_weight(early)
         for s in ids:
             states[s] = project_all(early, s, vec(bo_ref, layer), states[s])
             share(late, s, cross_attend(layer, s, states[s]))
             if layer + 1 < layers:
                 start_cross(layer + 1, s)
-            if s == 0 and layer == 0:
-                forward_weight(late)
+        forward_weight(late)
         finish_weight(late)
-        if layer + 1 < layers:
-            spread_weight(early + 2)
-            spread_weight(late + 2)
         for s in ids:
             states[s] = project_all(late, s, vec(bco_ref, layer), states[s])
             scatter(layer, s, mlp(layer, states[s]), states[s])
         for s in ids:
             reduce_and_gather(layer, s, vec(b2_ref, layer))
         if layer + 1 < layers:
-            forward_weight(early + 2)
-            forward_weight(late + 2)
+            spread_weight(early + 2)
     for s in ids:
         hidden_out_ref[s * size:(s + 1) * size, :] = collect(layers - 1, s).astype(BF16)
     for copy in sends:

time: 81.7 us -> 74.1 us (0.907)
  Pallas kernels: 80.8 us -> 73.2 us
    pallas_call x1, Pallas kernels: 65.8 us -> 58.2 us  [run_layers(): pl.pallas_call(functools.partial(layers_kernel, layers, tp, group, cross_...]
where the time goes in v5:
time: 74.1 us; the launch traced here: 74 us
  Pallas kernels  73.2 us (99%)
  between operations  0.81 us (1%)
    pallas_call x1, Pallas kernels, run_layers(): pl.pallas_call(functools.partial(layers_kernel, layers, tp, group, cross_...  58.2 us
    pallas_call x1, Pallas kernels, write_caches(): pl.pallas_call(functools.partial(write_kernel, group, layers), out_shape=...  15 us

profile of v5, /device:TPU:113, one launch (start us, length us, event | category | flops | bytes accessed | tf_op | source)
XLA Modules:
  0.0 74.0 jit_solution(17758779585031906483)
XLA Ops:
  0.6 58.2 %decoder_layers.1 = (bf16[160,512]{1,0:T(8,128)(2,1)S(1)}, bf16[2,160,64]{2,1,0:T(8,128)(2,1)S(1)}, bf16[2,160,64]{2,1,0:T(8,128)(2,1)S(1)}, bf16[20,512,448]{2,...) custom-call(s32[160]{0:T(256)} %pos_hbm.1, ...), custom_call_target="tpu_custom_call" | custom-call | tf_op jit(solution)/shard_map/decoder_layers/pallas_call | solution.py:429
  58.9 15.0 %write_caches.1 = (bf16[160,512]{1,0:T(8,128)(2,1)}, bf16[20480,448]{1,0:T(8,128)(2,1)}, bf16[20480,448]{1,0:T(8,128)(2,1)}, bf16[20,512,448]{2,1,0:T(8,128)(2,1...) custom-call(s32[160]{0:T(256)} %pos_hbm.1, ...), custom_call_target="tpu_custom_call", output_to_operand_aliasing={{3}: (4, {}), {4}: (5, {}), {5}: (6, {}), {6}: (7, {})} | custom-call | tf_op jit(solution)/shard_map/write_caches/pallas_call | solution.py:134

commit v6 on v5

--- a/solution.py
+++ b/solution.py
@@ -383,10 +383,7 @@
                 start_cross(0, s)
             if s == 0:
                 spread_weight(late)
-                if layer:
-                    forward_weight(early)
-        if layer == 0:
-            forward_weight(early)
+        forward_weight(early)
         if layer + 1 < layers:
             for s in ids:
                 start_self(layer + 1, 0, s)

time: 74.1 us -> 73.7 us (level)
  no operation moved by 1% of the time
where the time goes in v6:
time: 73.7 us
  Pallas kernels  72.8 us (99%)
  between operations  0.81 us (1%)
    pallas_call x1, Pallas kernels, run_layers(): pl.pallas_call(functools.partial(layers_kernel, layers, tp, group, cross_...  57.9 us
    pallas_call x1, Pallas kernels, write_caches(): pl.pallas_call(functools.partial(write_kernel, group, layers), out_shape=...  15 us

profile of v6, /device:TPU:113, one launch (start us, length us, event | category | flops | bytes accessed | tf_op | source)
XLA Modules:
  0.0 73.7 jit_solution(13399410335467528528)
XLA Ops:
  0.6 57.9 %decoder_layers.1 = (bf16[160,512]{1,0:T(8,128)(2,1)S(1)}, bf16[2,160,64]{2,1,0:T(8,128)(2,1)S(1)}, bf16[2,160,64]{2,1,0:T(8,128)(2,1)S(1)}, bf16[20,512,448]{2,...) custom-call(s32[160]{0:T(256)} %pos_hbm.1, ...), custom_call_target="tpu_custom_call" | custom-call | tf_op jit(solution)/shard_map/decoder_layers/pallas_call | solution.py:426
  58.5 15.0 %write_caches.1 = (bf16[160,512]{1,0:T(8,128)(2,1)}, bf16[20480,448]{1,0:T(8,128)(2,1)}, bf16[20480,448]{1,0:T(8,128)(2,1)}, bf16[20,512,448]{2,1,0:T(8,128)(2,1...) custom-call(s32[160]{0:T(256)} %pos_hbm.1, ...), custom_call_target="tpu_custom_call", output_to_operand_aliasing={{3}: (4, {}), {4}: (5, {}), {5}: (6, {}), {6}: (7, {})} | custom-call | tf_op jit(solution)/shard_map/write_caches/pallas_call | solution.py:134
